TPU v7x, 32 devices: a 4x4x1 block of a 4x4x8 slice. The times are simulated.
32 devices in a mesh: data: 1 (over z), ep: 32 (over y, x, core).
Axes of the slice: x: 4, y: 4, z: 1, core: 2. Of those that a mesh axis runs over, the one named last changes fastest.
The devices are a block of a 4x4x8 slice.
Arguments:
- x_in: bfloat16 [32, 2048, 1024], P(('data', 'ep'))
- w_query: bfloat16 [1024, 16, 64], P('ep')
- w_keyval: bfloat16 [1024, 16, 64], P('ep')
- w_out: bfloat16 [1024, 1024], P('ep')
- attn_gain: bfloat16 [1024], replicated
- moe_gain: bfloat16 [1024], replicated
- w_gate: bfloat16 [32, 1024, 512], P(None, 'ep')
- w_up: bfloat16 [32, 1024, 512], P(None, 'ep')
- w_down: bfloat16 [32, 512, 1024], P(None, None, 'ep')
- expert_ids: int32 [32, 2048, 8], P(('data', 'ep'))
- slot_ids: int32 [32, 2048, 8], P(('data', 'ep'))
- fill_counts: int32 [32, 32], P(('data', 'ep'))
- route_weight: bfloat16 [32, 2048, 8], P(('data', 'ep'))
Outputs:
- output: bfloat16 [32, 2048, 1024], P(('data', 'ep'))
All inputs are finite; a program needn't handle non-finite values.
Results may differ from a plain program's by a relative error of at most 0.02.
Values are sent between devices in bfloat16 or wider.
A program may use at most 768 MiB of HBM per device.

v0:
```python
import jax
import jax.numpy as jnp
from jax import lax
from jax.sharding import PartitionSpec as P


def rms_norm(val, gain):
    v32 = val.astype(jnp.float32)
    scale = lax.rsqrt(jnp.mean(v32 * v32, axis=-1, keepdims=True) + 1e-6)
    return (v32 * scale * gain.astype(jnp.float32)).astype(jnp.bfloat16)


def rotary(vals, cos_tab, sin_tab):
    half_dim = vals.shape[-1] // 2
    v32 = vals.astype(jnp.float32)
    first = v32[..., :half_dim]
    second = v32[..., half_dim:]
    return jnp.concatenate([first * cos_tab - second * sin_tab, second * cos_tab + first * sin_tab], axis=-1).astype(jnp.bfloat16)


def attention_block(x_in, w_query, w_keyval, w_out, attn_gain):
    batch_loc, seq_len, model_dim = x_in.shape
    num_heads, head_dim = w_query.shape[1], w_query.shape[2]
    kv_heads = w_keyval.shape[1] // 2
    groups = num_heads // kv_heads
    half_dim = head_dim // 2
    normed = rms_norm(x_in, attn_gain)
    query = jnp.einsum('bsd,dhk->bshk', normed, w_query, preferred_element_type=jnp.float32).astype(jnp.bfloat16)
    keyval = jnp.einsum('bsd,dhk->bshk', normed, w_keyval, preferred_element_type=jnp.float32).astype(jnp.bfloat16)
    inv_freq = 10000.0 ** (-jnp.arange(half_dim, dtype=jnp.float32) / half_dim)
    angles = jnp.arange(seq_len, dtype=jnp.float32)[:, None] * inv_freq[None, :]
    cos_tab = jnp.cos(angles)[None, :, None, :]
    sin_tab = jnp.sin(angles)[None, :, None, :]
    query = rotary(query, cos_tab, sin_tab).reshape(batch_loc, seq_len, kv_heads, groups, head_dim)
    keys = rotary(keyval[:, :, :kv_heads], cos_tab, sin_tab)
    values = keyval[:, :, kv_heads:]
    scores = jnp.einsum('bqhgk,bshk->bhgqs', query, keys, preferred_element_type=jnp.float32) * (head_dim ** -0.5)
    causal = jnp.arange(seq_len)[:, None] >= jnp.arange(seq_len)[None, :]
    scores = jnp.where(causal, scores, -1e30)
    attn_prob = jax.nn.softmax(scores, axis=-1).astype(jnp.bfloat16)
    mixed = jnp.einsum('bhgqs,bshk->bqhgk', attn_prob, values, preferred_element_type=jnp.float32).astype(jnp.bfloat16)
    attn_out = jnp.einsum('crg,ge->cre', mixed.reshape(batch_loc, seq_len, num_heads * head_dim), w_out, preferred_element_type=jnp.float32)
    return (x_in.astype(jnp.float32) + attn_out).astype(jnp.bfloat16)


def pack_rows(u_rows, ids, slots, counts, experts, capacity):
    tokens, choices = ids.shape
    count_at = jnp.take(counts.reshape(-1), ids)
    flat_pos = jnp.where(slots < count_at, ids * capacity + slots, experts * capacity)
    tok_ids = jnp.broadcast_to(jnp.arange(tokens, dtype=jnp.int32)[:, None], (tokens, choices))
    slot_owner = jnp.full((experts * capacity + 1,), tokens, jnp.int32).at[flat_pos.reshape(-1)].set(tok_ids.reshape(-1))
    packed = jnp.take(u_rows, slot_owner[:experts * capacity], axis=0, mode='fill', fill_value=0)
    return packed.reshape(experts, capacity, u_rows.shape[-1]), flat_pos


def combine_rows(h_rows, back, flat_pos, gate_rows):
    experts, capacity, model_dim = back.shape
    picked = jnp.take(back.reshape(experts * capacity, model_dim), flat_pos, axis=0, mode='fill', fill_value=0)
    mix_sum = jnp.einsum('tk,tkd->td', gate_rows, picked, preferred_element_type=jnp.float32)
    return (h_rows.astype(jnp.float32) + mix_sum).astype(jnp.bfloat16)


def expert_ffn(in_rows, w_gate, w_up, w_down):
    act_gate = jnp.einsum('ecd,edf->ecf', in_rows, w_gate, preferred_element_type=jnp.float32)
    act_up = jnp.einsum('ecd,edf->ecf', in_rows, w_up, preferred_element_type=jnp.float32)
    hidden_mid = (jax.nn.silu(act_gate) * act_up).astype(jnp.bfloat16)
    return jnp.einsum('ecf,efd->ecd', hidden_mid, w_down, preferred_element_type=jnp.float32).astype(jnp.bfloat16)


def solution(mesh):
    row_spec = P(('data', 'ep'))

    def device_step(x_in, w_query, w_keyval, w_out, attn_gain, moe_gain, w_gate, w_up, w_down, expert_ids, slot_ids, fill_counts, route_weight):
        full_query = lax.all_gather(w_query, 'ep', axis=0, tiled=True)
        full_keyval = lax.all_gather(w_keyval, 'ep', axis=0, tiled=True)
        full_out = lax.all_gather(w_out, 'ep', axis=0, tiled=True)
        hidden = attention_block(x_in, full_query, full_keyval, full_out, attn_gain)
        own_gate = lax.all_to_all(w_gate, 'ep', 0, 1, tiled=True)
        own_up = lax.all_to_all(w_up, 'ep', 0, 1, tiled=True)
        own_down = lax.all_to_all(w_down, 'ep', 0, 2, tiled=True)
        batch_loc, seq_len, model_dim = x_in.shape
        experts = w_gate.shape[0]
        choices = expert_ids.shape[-1]
        tokens = batch_loc * seq_len
        capacity = 2 * tokens * choices // experts
        h_rows = hidden.reshape(tokens, model_dim)
        u_rows = rms_norm(h_rows, moe_gain)
        packed, flat_pos = pack_rows(u_rows, expert_ids.reshape(tokens, choices), slot_ids.reshape(tokens, choices), fill_counts, experts, capacity)
        received = lax.all_to_all(packed, 'ep', 0, 1, tiled=True)
        result = expert_ffn(received, own_gate, own_up, own_down)
        back = lax.all_to_all(result, 'ep', 1, 0, tiled=True)
        out_rows = combine_rows(h_rows, back, flat_pos, route_weight.reshape(tokens, choices))
        return out_rows.reshape(batch_loc, seq_len, model_dim)

    in_specs = (row_spec, P('ep'), P('ep'), P('ep'), P(), P(), P(None, 'ep'), P(None, 'ep'), P(None, None, 'ep'), row_spec, row_spec, row_spec, row_spec)
    return jax.shard_map(device_step, mesh=mesh, in_specs=in_specs, out_specs=row_spec, check_vma=False)
```

profile of v0, /device:TPU:118, one launch (start us, length us, event | category | flops | bytes accessed | tf_op | source)
XLA Modules:
  0.0 3659.2 jit_solution(651846055918736767)
XLA Ops:
  9.9 6.6 all-to-all-start.1
  17.4 4.1 iota_compare_fusion
  25.5 6.5 copy.50
  32.0 3.1 fusion.4
  38.2 21.1 compare_and_fusion.1
  62.0 60.6 %scatter_custom_fusion = s32[32769]{0:T(1024)S(1)} fusion(s32[16384]{0:T(1024)S(1)} %bitcast.315, s32[16384]{0:T(1024)S(1)} %reshape.523, s32[]{:T(128)} %constant.72.clone.1), kind=kCustom, calls=%fused_computation.66 | custom fusion | bytes 131080 | tf_op jit(solution)/shard_map/scatter | solution.py:51
  123.9 8.4 convert_bitcast_fusion.1
  136.9 8.3 bitcast_convert_fusion
  148.0 86.8 %fusion.1 = (f32[8,2,2048]{2,1,0:T(2,128)S(1)}, f32[8,2048,2048,2]{2,1,3,0:T(8,128)}) fusion(pred[2048,2048]{0,1:T(8,128)(4,1)S(1)} %copy-done, bf16[2048,8,2,32]{0,3,2,1:T(8,128)(2,1)} %bitcast.312, bf16[2048,8,2,32]{0,3,2,1:T(8,128)(2,1)S(1)} %bitcast.311, bf16[2048,8,32]{0,2,1:T(8,128)(2,1)} %get-tuple-element.10, bf16[2048,8,32]{0,2,1:T(8,128)(2,1)} %get-tuple-element.9), kind=kOutput, calls=%fused_computation.7 | convolution fusion | flops 8803811328 | bytes 279052288 | tf_op jit(solution)/shard_map/bqhgk,bshk->bhgqs/dot_general | solution.py:37
  234.8 82.0 %fusion = f32[8,2,2048]{2,1,0:T(2,128)S(1)} fusion(f32[8,2048,2048,2]{2,1,3,0:T(8,128)} %get-tuple-element.48, f32[8,2,2048]{2,1,0:T(2,128)S(1)} %get-tuple-element.47, pred[2048,2048]{0,1:T(8,128)(4,1)} %iota_compare_fusion), kind=kLoop, calls=%fused_computation.6 | loop fusion | flops 268402688 | bytes 272891904 | tf_op jit(solution)/shard_map/reduce_sum | solution.py:40
  316.8 87.8 %fusion.18 = bf16[8,64,2,2048]{3,1,2,0:T(8,128)(2,1)} fusion(f32[8,2,2048]{2,1,0:T(2,128)S(1)} %fusion, f32[8,2,2048]{2,1,0:T(2,128)S(1)} %get-tuple-element.47, f32[8,2048,2048,2]{2,1,3,0:T(8,128)} %get-tuple-element.48, pred[2048,2048]{0,1:T(8,128)(4,1)} %iota_compare_fusion, bf16[1,2048,16,64]{1,3,2,0:T(8,128)(2,1)} %copy-done.5), kind=kOutput, calls=%fused_computation.41 | convolution fusion | flops 8927576064 | bytes 279183360 | tf_op jit(solution)/shard_map/bhgqs,bshk->bqhgk/dot_general | solution.py:41
  404.6 9.2 fusion.8
  418.8 6.4 copy.60
  425.2 161.5 %gather_fusion = bf16[32768,1024]{1,0:T(8,128)(2,1)} fusion(bf16[2048,1024]{1,0:T(8,128)(2,1)} %copy.60, s32[32768]{0:T(1024)S(1)} %copy-done.12), kind=kCustom, calls=%fused_computation | custom fusion | bytes 134348800 | tf_op jit(solution)/shard_map/jit(_take)/gather | solution.py:52
  586.7 6.3 all-to-all-start.2
  593.1 44.0 %broadcast_select_fusion = bf16[32,1024,1024]{2,1,0:T(8,128)(2,1)} fusion(bf16[32,1024,1024]{2,1,0:T(8,128)(2,1)} %bitcast.86, pred[32,1024]{1,0:T(8,128)(4,1)S(1)} %copy-done.13), kind=kLoop, calls=%fused_computation.14 | loop fusion | flops 33554432 | bytes 134250496 | tf_op jit(solution)/shard_map/jit(_take)/select_n | solution.py:52
  637.1 825.7 %all_to_all.51 = bf16[32,1024,1024]{2,1,0:T(8,128)(2,1)} all-to-all(bf16[32,1024,1024]{2,1,0:T(8,128)(2,1)} %broadcast_select_fusion), channel_id=1, replica_groups=mesh['data'=1,'ep'=32] {'ep'}, dimensions={0} | all-to-all | bytes 134217728 | tf_op jit(solution)/shard_map/all_to_all | solution.py:89
  1462.7 25.6 all-to-all-start.3
  1488.3 58.0 %fusion.62 = f32[32768,512]{1,0:T(8,128)} fusion(bf16[32768,1024]{1,0:T(8,128)(2,1)} %bitcast.87, bf16[1024,512]{1,0:T(8,128)(2,1)} %bitcast.88), kind=kOutput, calls=%fused_computation.112 | convolution fusion | flops 34359738368 | bytes 135266304 | tf_op jit(solution)/shard_map/ecd,edf->ecf/dot_general | solution.py:64
  1546.2 87.4 %convert_bitcast_fusion = bf16[1,32768,1024]{2,1,0:T(8,128)(2,1)} fusion(bf16[512,1024]{0,1:T(8,128)(2,1)S(1)} %bitcast.314, f32[32768,512]{1,0:T(8,128)} %fusion.62, bf16[32768,1024]{1,0:T(8,128)(2,1)} %bitcast.87, bf16[1024,512]{1,0:T(8,128)(2,1)S(1)} %bitcast.313), kind=kOutput, calls=%fused_computation.12 | convolution fusion | flops 68853694464 | bytes 203423744 | tf_op jit(solution)/shard_map/ecf,efd->ecd/dot_general | solution.py:67
  1633.7 111.5 %copy.80 = bf16[1,32768,1024]{2,0,1:T(2,128)(2,1)} copy(bf16[1,32768,1024]{2,1,0:T(8,128)(2,1)} %convert_bitcast_fusion) | data formatting | bytes 134217728 | tf_op jit(solution)/shard_map/convert_element_type | solution.py:67
  1745.7 389.3 %reduce.5 = bf16[32768,1024]{1,0:T(8,128)(2,1)} reduce(bf16[32768,1,1024]{2,1,0:T(2,128)(2,1)} %bitcast.310, bf16[]{:T(256)} %broadcast.541), dimensions={1}, to_apply=%bitcast.310.reduce_sub_computation | reduce | bytes 134217728
  2135.0 65.6 %reshape.683 = bf16[32,2,524288]{2,1,0:T(2,128)(2,1)} reshape(bf16[32768,1024]{1,0:T(8,128)(2,1)} %reduce.5) | data formatting | bytes 134217728
  2200.6 7.1 all-to-all-start.4
  2211.0 890.3 %all-to-all-done.4 = bf16[32,2,524288]{2,1,0:T(2,128)(2,1)} async-done(((bf16[32,2,524288]{2,1,0:T(2,128)(2,1)}), bf16[32,2,524288]{2,1,0:T(2,128)(2,1)}, u32[]{:S(2)}, u32[]{:S(2)}) %all-to-all-start.4) | async-done | bytes 67108896 | tf_op jit(solution)/shard_map/all_to_all | solution.py:91
  3101.4 82.6 %reshape.684 = bf16[32768,1,1024]{2,1,0:T(2,128)(2,1)} reshape(bf16[32,2,524288]{2,1,0:T(2,128)(2,1)} %all-to-all-done.4) | data formatting | bytes 134217728
  3183.9 65.0 %copy.79 = bf16[1,32768,1024]{2,1,0:T(8,128)(2,1)} copy(bf16[1,32768,1024]{2,0,1:T(2,128)(2,1)} %bitcast.254) | data formatting | bytes 134217728
  3248.9 344.6 %gather_fusion.1 = bf16[16384,1024]{1,0:T(8,128)(2,1)} fusion(bf16[32768,1024]{1,0:T(8,128)(2,1)} %bitcast.309, s32[16384]{0:T(1024)S(1)} %broadcast_clamp_fusion), kind=kCustom, calls=%fused_computation.1 | custom fusion | bytes 67174400 | tf_op jit(solution)/shard_map/jit(_take)/gather | solution.py:58
  3593.6 34.8 multiply_reduce_fusion
  3628.4 9.2 copy.72
  3637.6 8.3 fusion.12
  3645.8 6.4 copy.63
  (84 shorter events, 31.3 us)
Async XLA Ops:
  6.5 117.4 %all-gather.4.cloned.1.call-start = ((), (), s32[]{:S(2)}) async-start(), calls=%async_computation.5 | async-start | bytes 4325376 | tf_op jit(solution)/shard_map/all_gather | solution.py:75
  8.2 128.7 %all-gather.6.cloned.1.call-start = ((), (), s32[]{:S(2)}) async-start(), calls=%async_computation.6 | async-start | bytes 4325376 | tf_op jit(solution)/shard_map/all_gather | solution.py:74
  9.9 576.8 %all-to-all-start.1 = ((bf16[32,32,512]{2,1,0:T(8,128)(2,1)}), bf16[32,32,512]{2,1,0:T(8,128)(2,1)}, u32[]{:S(2)}, u32[]{:S(2)}) async-start(bf16[32,32,512]{2,1,0:T(8,128)(2,1)} %param.19), calls=%async_computation.1 | async-start | bytes 2097152 | tf_op jit(solution)/shard_map/all_to_all | solution.py:78
  16.6 388.0 %all-gather.8.cloned.1.call-start = ((), (), s32[]{:S(2)}) async-start(), calls=%async_computation.7 | async-start | bytes 2162688 | tf_op jit(solution)/shard_map/all_gather | solution.py:76
  17.4 17.7 copy-start.17
  17.4 19.5 copy-start.18
  17.4 20.1 copy-start.6
  17.4 20.4 copy-start.8
  59.2 73.1 %copy-start.10 = (s32[2048,8]{0,1:T(8,128)}, s32[2048,8]{0,1:T(8,128)S(1)}, u32[]{:S(2)}) copy-start(s32[2048,8]{0,1:T(8,128)S(1)} %get-tuple-element.6) | copy-start | bytes 196612
  123.9 11.0 copy-start.3
  132.4 2.0 copy-start.5
  145.2 2.8 copy-start
  404.6 11.2 copy-start.16
  413.8 2.0 copy-start.1
  415.8 9.4 copy-start.12
  425.2 167.9 %copy-start.13 = (pred[32,1024]{1,0:T(8,128)(4,1)S(1)}, pred[32,1024]{1,0:T(8,128)(4,1)}, u32[]{:S(2)}) copy-start(pred[32,1024]{1,0:T(8,128)(4,1)} %compare_and_fusion) | copy-start | bytes 98308
  586.7 50.4 %all-to-all-start.2 = ((bf16[32,32,512]{2,1,0:T(8,128)(2,1)}), bf16[32,32,512]{2,1,0:T(8,128)(2,1)S(1)}, u32[]{:S(2)}, u32[]{:S(2)}) async-start(bf16[32,32,512]{2,1,0:T(8,128)(2,1)} %param.20), calls=%async_computation.2 | async-start | bytes 2097152 | tf_op jit(solution)/shard_map/all_to_all | solution.py:79
  1462.7 83.5 %all-to-all-start.3 = ((bf16[32,512,32]{1,2,0:T(8,128)(2,1)}), bf16[32,512,32]{1,2,0:T(8,128)(2,1)S(1)}, u32[]{:S(2)}, u32[]{:S(2)}) async-start(bf16[32,512,32]{1,2,0:T(8,128)(2,1)} %param.21), calls=%async_computation.3 | async-start | bytes 2097152 | tf_op jit(solution)/shard_map/all_to_all | solution.py:80
  2200.6 7.1 copy-start.7
  2200.6 7.1 copy-start.9
  2200.6 7.1 copy-start.11
  2200.6 8.0 copy-start.14
  2200.6 9.1 copy-start.15
  2200.6 900.7 %all-to-all-start.4 = ((bf16[32,2,524288]{2,1,0:T(2,128)(2,1)}), bf16[32,2,524288]{2,1,0:T(2,128)(2,1)}, u32[]{:S(2)}, u32[]{:S(2)}) async-start(bf16[32,2,524288]{2,1,0:T(2,128)(2,1)} %reshape.683), calls=%async_computation.4 | async-start | bytes 134217728 | tf_op jit(solution)/shard_map/all_to_all | solution.py:91
  3248.9 344.6 %copy-start.2 = (f32[2048,8]{1,0:T(8,128)S(1)}, f32[2048,8]{1,0:T(8,128)}, u32[]{:S(2)}) copy-start(f32[2048,8]{1,0:T(8,128)} %copy.76) | copy-start | bytes 196612
  3248.9 344.6 %copy-start.4 = (pred[2048,8]{1,0:T(8,128)(4,1)S(1)}, pred[2048,8]{1,0:T(8,128)(4,1)}, u32[]{:S(2)}) copy-start(pred[2048,8]{1,0:T(8,128)(4,1)} %copy.56) | copy-start | bytes 49156
Sparse Core Ops, SparseCore 0:
  9.3 48.0 all-gather.3
  59.4 42.5 all-gather.5
  104.1 37.5 all-gather.7
where the time goes:
time: 3680 us; the launch traced here: 3660 us
  local copies, waits for them, and re-layouts  938 us (25%)
  waiting for transfers between devices  891 us (24%)
  blocking collectives  826 us (22%)
  other arithmetic  599 us (16%)
  matrix products  346 us (9%)
  starting transfers between devices  45.8 us (1%)
    all_to_all x1, waiting for transfers between devices, device_step(): back = lax.all_to_all(result, 'ep', 1, 0, tiled=True)  890 us
    all_to_all x1, blocking collectives, device_step(): received = lax.all_to_all(packed, 'ep', 0, 1, tiled=True)  826 us
    unnamed x3, other arithmetic  424 us
    gather x1, local copies, waits for them, and re-layouts, combine_rows(): jnp.take(back.reshape(experts * capacity, model_dim), flat_pos, axis=0, m...  345 us
    unnamed x48, local copies, waits for them, and re-layouts  229 us
    gather x1, local copies, waits for them, and re-layouts, pack_rows(): jnp.take(u_rows, slot_owner[:experts * capacity], axis=0, mode='fill', fi...  162 us
    convert_element_type x1, local copies, waits for them, and re-layouts, expert_ffn(): jnp.einsum('ecf,efd->ecd', hidden_mid, w_down, preferred_element_type=jnp...  112 us
    dot_general x1, matrix products, attention_block(): jnp.einsum('bhgqs,bshk->bqhgk', attn_prob, values, preferred_element_type...  87.8 us
  transfers between devices with their start and end apart: 7, of which 1 were waited for; matrix products, arithmetic and copies ran while one was open for 18% of the time, Pallas kernels for 0%

commit v1 on v0

v1 whole, which is shorter than its diff:
```python
import functools

import jax
import jax.numpy as jnp
from jax import lax
from jax.experimental import pallas as pl
from jax.experimental.pallas import tpu as pltpu
from jax.sharding import PartitionSpec as P

LANES = 128
QKV_ROWS = 256
ATT_ROWS = 512
OUT_ROWS = 256
MOE_ROWS = 512
CHUNKS = 4
BIG_VMEM = 60 * 1024 * 1024


def f32dot(lhs, rhs):
    return jnp.dot(lhs, rhs, preferred_element_type=jnp.float32)


def f32dot_t(lhs, rhs):
    return lax.dot_general(lhs, rhs, (((1,), (1,)), ((), ())), preferred_element_type=jnp.float32)


def rms_rows(v32, gain):
    scale = lax.rsqrt(jnp.mean(v32 * v32, axis=-1, keepdims=True) + 1e-6)
    return (v32 * scale * gain).astype(jnp.bfloat16)


def resident(shape, index_map):
    return pl.BlockSpec(shape, index_map, pipeline_mode=pl.Buffered(1))


def qkv_kernel(head_dim, q_cols, k_cols, x_ref, gain_ref, w_ref, cos_ref, sin_ref, q_ref, kk_ref, vv_ref):
    half_dim = head_dim // 2
    normed = rms_rows(x_ref[...].astype(jnp.float32), gain_ref[...].astype(jnp.float32))
    cos_tab = cos_ref[...]
    sin_tab = sin_ref[...]
    rows = x_ref.shape[0]
    lane = lax.broadcasted_iota(jnp.int32, (rows, LANES), 1)
    low_half = lax.rem(lane, head_dim) < half_dim

    def rotated(vals):
        v32 = vals.astype(jnp.bfloat16).astype(jnp.float32)
        other = jnp.where(low_half, pltpu.roll(v32, LANES - half_dim, 1), pltpu.roll(v32, half_dim, 1))
        return v32 * cos_tab + other * sin_tab

    query = f32dot(normed, w_ref[:, :q_cols])
    for c in range(q_cols // LANES):
        cols = slice(c * LANES, (c + 1) * LANES)
        q_ref[:, cols] = rotated(query[:, cols]).astype(jnp.bfloat16)
    keys = f32dot(normed, w_ref[:, q_cols:q_cols + k_cols])
    for c in range(k_cols // LANES):
        cols = slice(c * LANES, (c + 1) * LANES)
        rot = rotated(keys[:, cols]).astype(jnp.bfloat16).astype(jnp.float32)
        kk_ref[0, :, cols] = rot.astype(jnp.bfloat16)
        kk_ref[1, :, cols] = pltpu.roll(rot, head_dim, 1).astype(jnp.bfloat16)
    values = f32dot(normed, w_ref[:, q_cols + k_cols:])
    for c in range(k_cols // LANES):
        cols = slice(c * LANES, (c + 1) * LANES)
        val = values[:, cols].astype(jnp.bfloat16).astype(jnp.float32)
        vv_ref[0, :, cols] = val.astype(jnp.bfloat16)
        vv_ref[1, :, cols] = pltpu.roll(val, head_dim, 1).astype(jnp.bfloat16)


def qkv_call(x_rows, gain, w_qkv, cos_tab, sin_tab, head_dim, q_cols, k_cols):
    tokens, width = x_rows.shape
    rows = QKV_ROWS
    return pl.pallas_call(
        functools.partial(qkv_kernel, head_dim, q_cols, k_cols),
        grid=(tokens // rows,),
        in_specs=[
            pl.BlockSpec((rows, width), lambda i: (i, 0)),
            resident((1, width), lambda i: (0, 0)),
            resident(w_qkv.shape, lambda i: (0, 0)),
            pl.BlockSpec((rows, LANES), lambda i: (i, 0)),
            pl.BlockSpec((rows, LANES), lambda i: (i, 0)),
        ],
        out_specs=[
            pl.BlockSpec((rows, q_cols), lambda i: (i, 0)),
            pl.BlockSpec((2, rows, k_cols), lambda i: (0, i, 0)),
            pl.BlockSpec((2, rows, k_cols), lambda i: (0, i, 0)),
        ],
        out_shape=[
            jax.ShapeDtypeStruct((tokens, q_cols), jnp.bfloat16),
            jax.ShapeDtypeStruct((2, tokens, k_cols), jnp.bfloat16),
            jax.ShapeDtypeStruct((2, tokens, k_cols), jnp.bfloat16),
        ],
        compiler_params=pltpu.CompilerParams(vmem_limit_bytes=BIG_VMEM),
        cost_estimate=pl.CostEstimate(flops=2 * tokens * width * w_qkv.shape[1], bytes_accessed=tokens * width * 10, transcendentals=0),
        name='qkv_rope',
    )(x_rows, gain, w_qkv, cos_tab, sin_tab)


def attend_kernel(head_dim, q_ref, ka_ref, kb_ref, va_ref, vb_ref, o_ref, s_buf, m_buf, l_buf, o_buf):
    rows = q_ref.shape[0]
    step = pl.program_id(1)
    lane = lax.broadcasted_iota(jnp.int32, (rows, LANES), 1)
    low = lane < head_dim
    query = q_ref[...].astype(jnp.float32) * (head_dim ** -0.5)
    zero = jnp.zeros_like(query)
    heads = (jnp.where(low, query, zero).astype(jnp.bfloat16), jnp.where(low, zero, query).astype(jnp.bfloat16))
    key_refs = (ka_ref, kb_ref)
    val_refs = (va_ref, vb_ref)
    groups = rows // LANES

    def span(blk):
        return pl.ds(pl.multiple_of(blk * rows, rows), rows)

    def fold(op, tile):
        out = tile[:, :LANES]
        for g in range(1, groups):
            out = op(out, tile[:, g * LANES:(g + 1) * LANES])
        return out

    def scores(head, blk, masked):
        tile = f32dot_t(heads[head], key_refs[head][0, span(blk), :])
        if masked:
            row_id = lax.broadcasted_iota(jnp.int32, (rows, rows), 0)
            col_id = lax.broadcasted_iota(jnp.int32, (rows, rows), 1)
            tile = jnp.where(row_id >= col_id, tile, -1e30)
        s_buf[head, :, span(blk)] = tile
        m_buf[head] = jnp.maximum(m_buf[head], fold(jnp.maximum, tile))

    def exps(head, blk, row_max):
        tile = jnp.exp(s_buf[head, :, span(blk)] - row_max)
        s_buf[head, :, span(blk)] = tile
        l_buf[head] += fold(jnp.add, tile)

    def mixes(head, blk, inv_sum):
        prob = (s_buf[head, :, span(blk)] * inv_sum).astype(jnp.bfloat16)
        o_buf[head] += f32dot(prob, val_refs[head][0, span(blk), :])

    m_buf[...] = jnp.full_like(m_buf, -1e30)
    l_buf[...] = jnp.zeros_like(l_buf)
    o_buf[...] = jnp.zeros_like(o_buf)

    @pl.loop(0, step)
    def _(blk):
        scores(0, blk, False)

    scores(0, step, True)
    max0 = jnp.max(m_buf[0], axis=-1, keepdims=True)

    @pl.loop(0, step)
    def _(blk):
        scores(1, blk, False)
        exps(0, blk, max0)

    scores(1, step, True)
    exps(0, step, max0)
    max1 = jnp.max(m_buf[1], axis=-1, keepdims=True)
    inv0 = 1.0 / jnp.sum(l_buf[0], axis=-1, keepdims=True)

    @pl.loop(0, step + 1)
    def _(blk):
        mixes(0, blk, inv0)
        exps(1, blk, max1)

    inv1 = 1.0 / jnp.sum(l_buf[1], axis=-1, keepdims=True)

    @pl.loop(0, step + 1)
    def _(blk):
        mixes(1, blk, inv1)

    o_ref[...] = jnp.where(low, o_buf[0], o_buf[1]).astype(jnp.bfloat16)


def attend_call(query, keys, values, head_dim):
    tokens, q_cols = query.shape
    kv_heads = keys.shape[2] // head_dim
    rows = min(ATT_ROWS, tokens)
    per_tile = LANES // head_dim
    kv_block = (1, tokens, LANES)
    same = lambda h, i: (h % per_tile, 0, h // per_tile)
    other = lambda h, i: (1 - h % per_tile, 0, h // per_tile)
    return pl.pallas_call(
        functools.partial(attend_kernel, head_dim),
        grid=(kv_heads, tokens // rows),
        in_specs=[
            pl.BlockSpec((rows, LANES), lambda h, i: (i, h)),
            pl.BlockSpec(kv_block, same),
            pl.BlockSpec(kv_block, other),
            pl.BlockSpec(kv_block, same),
            pl.BlockSpec(kv_block, other),
        ],
        out_specs=pl.BlockSpec((rows, LANES), lambda h, i: (i, h)),
        out_shape=jax.ShapeDtypeStruct((tokens, q_cols), jnp.bfloat16),
        scratch_shapes=[
            pltpu.VMEM((2, rows, tokens), jnp.float32),
            pltpu.VMEM((2, rows, LANES), jnp.float32),
            pltpu.VMEM((2, rows, LANES), jnp.float32),
            pltpu.VMEM((2, rows, LANES), jnp.float32),
        ],
        compiler_params=pltpu.CompilerParams(vmem_limit_bytes=BIG_VMEM),
        cost_estimate=pl.CostEstimate(flops=8 * tokens * tokens * q_cols, bytes_accessed=tokens * q_cols * 12, transcendentals=tokens * tokens * q_cols // LANES),
        name='attend',
    )(query, keys, keys, values, values)


def out_kernel(mixed_ref, w_ref, x_ref, gain_ref, h_ref, u_ref):
    hidden = (x_ref[...].astype(jnp.float32) + f32dot(mixed_ref[...], w_ref[...])).astype(jnp.bfloat16)
    h_ref[...] = hidden
    u_ref[...] = rms_rows(hidden.astype(jnp.float32), gain_ref[...].astype(jnp.float32))


def out_call(mixed, w_out, x_rows, gain):
    tokens, width = x_rows.shape
    rows = OUT_ROWS
    block = pl.BlockSpec((rows, width), lambda i: (i, 0))
    return pl.pallas_call(
        out_kernel,
        grid=(tokens // rows,),
        in_specs=[
            pl.BlockSpec((rows, mixed.shape[1]), lambda i: (i, 0)),
            resident(w_out.shape, lambda i: (0, 0)),
            block,
            resident((1, width), lambda i: (0, 0)),
        ],
        out_specs=[block, block],
        out_shape=[jax.ShapeDtypeStruct((tokens, width), jnp.bfloat16)] * 2,
        compiler_params=pltpu.CompilerParams(vmem_limit_bytes=BIG_VMEM),
        cost_estimate=pl.CostEstimate(flops=2 * tokens * width * mixed.shape[1], bytes_accessed=tokens * width * 10, transcendentals=0),
        name='out_proj',
    )(mixed, w_out, x_rows, gain)


def moe_kernel(first_expert, is_first, is_last, u_ref, gate_ref, w_ref, *rest):
    if is_first:
        rest = (None,) + rest
    acc_in, *rest = rest
    if is_last:
        h_ref, out_ref, acc, sem = rest
    else:
        out_ref, acc, sem = rest
    step = pl.program_id(0)
    expert = first_expert + step
    shards, _, _, depth, inner = w_ref.shape
    full = shards * depth

    @pl.when(step == 0)
    def _():
        if is_first:
            acc[...] = jnp.zeros_like(acc)
        else:
            copy = pltpu.make_async_copy(acc_in, acc, sem)
            copy.start()
            copy.wait()

    w_gate = w_ref[:, 0, 0].reshape(full, inner)
    w_up = w_ref[:, 1, 0].reshape(full, inner)
    w_down = w_ref[:, 2, 0].reshape(full, inner)
    tokens = u_ref.shape[0]

    @pl.loop(0, tokens // MOE_ROWS)
    def _(blk):
        rows = pl.ds(pl.multiple_of(blk * MOE_ROWS, MOE_ROWS), MOE_ROWS)
        in_rows = u_ref[rows, :]
        hidden_mid = (jax.nn.silu(f32dot(in_rows, w_gate)) * f32dot(in_rows, w_up)).astype(jnp.bfloat16)
        y_rows = f32dot_t(hidden_mid, w_down).astype(jnp.bfloat16).astype(jnp.float32)
        gates = gate_ref[rows, :]
        lane = lax.broadcasted_iota(jnp.int32, gates.shape, 1)
        weight = jnp.sum(jnp.where(lane == expert, gates, 0.0), axis=-1, keepdims=True)
        acc[rows, :] += jnp.where(weight > 0, weight * y_rows, 0.0)

    @pl.when(step == pl.num_programs(0) - 1)
    def _():
        if is_last:
            @pl.loop(0, tokens // MOE_ROWS)
            def _(blk):
                rows = pl.ds(pl.multiple_of(blk * MOE_ROWS, MOE_ROWS), MOE_ROWS)
                out_ref[rows, :] = (h_ref[rows, :].astype(jnp.float32) + acc[rows, :]).astype(jnp.bfloat16)
        else:
            copy = pltpu.make_async_copy(acc, out_ref, sem)
            copy.start()
            copy.wait()


def moe_call(u_rows, gates, weights, acc, h_rows, first_expert, is_last):
    tokens, width = u_rows.shape
    shards, parts, count, depth, inner = weights.shape
    is_first = acc is None
    whole = lambda e: (0, 0)
    args = [u_rows, gates, weights]
    in_specs = [
        resident((tokens, width), whole),
        resident(gates.shape, whole),
        pl.BlockSpec((shards, parts, 1, depth, inner), lambda e: (0, 0, e, 0, 0)),
    ]
    aliases = {}
    if not is_first:
        args.append(acc)
        in_specs.append(pl.BlockSpec(memory_space=pl.ANY))
        if not is_last:
            aliases = {3: 0}
    if is_last:
        args.append(h_rows)
        in_specs.append(resident((tokens, width), whole))
        out_spec = resident((tokens, width), whole)
        out_shape = jax.ShapeDtypeStruct((tokens, width), jnp.bfloat16)
    else:
        out_spec = pl.BlockSpec(memory_space=pl.ANY)
        out_shape = jax.ShapeDtypeStruct((tokens, width), jnp.float32)
    return pl.pallas_call(
        functools.partial(moe_kernel, first_expert, is_first, is_last),
        grid=(count,),
        in_specs=in_specs,
        out_specs=out_spec,
        out_shape=out_shape,
        scratch_shapes=[pltpu.VMEM((tokens, width), jnp.float32), pltpu.SemaphoreType.DMA],
        input_output_aliases=aliases,
        compiler_params=pltpu.CompilerParams(vmem_limit_bytes=BIG_VMEM),
        cost_estimate=pl.CostEstimate(flops=6 * tokens * width * inner * count, bytes_accessed=2 * weights.size + 16 * tokens * width, transcendentals=tokens * inner * count),
        name='moe_part',
    )(*args)


def gate_table(expert_ids, slot_ids, counts, weights):
    tokens, choices = expert_ids.shape
    limits = jnp.pad(counts, (0, LANES - counts.shape[0]))[None, :]
    lane = lax.broadcasted_iota(jnp.int32, (tokens, LANES), 1)
    table = jnp.zeros((tokens, LANES), jnp.float32)
    for k in range(choices):
        kept = (expert_ids[:, k:k + 1] == lane) & (slot_ids[:, k:k + 1] < limits)
        table = jnp.where(kept, weights[:, k:k + 1].astype(jnp.float32), table)
    return table


def local_layer(x_rows, w_qkv, w_out, attn_gain, moe_gain, expert_parts, gates, head_dim, q_cols, k_cols):
    tokens, width = x_rows.shape
    half_dim = head_dim // 2
    inv_freq = 10000.0 ** (-jnp.arange(half_dim, dtype=jnp.float32) / half_dim)
    angles = jnp.arange(tokens, dtype=jnp.float32)[:, None] * inv_freq[None, :]
    cos_half, sin_half = jnp.cos(angles), jnp.sin(angles)
    reps = LANES // head_dim
    cos_tab = jnp.tile(cos_half, (1, 2 * reps))
    sin_tab = jnp.tile(jnp.concatenate([-sin_half, sin_half], axis=1), (1, reps))
    query, keys, values = qkv_call(x_rows, attn_gain[None, :], w_qkv, cos_tab, sin_tab, head_dim, q_cols, k_cols)
    mixed = attend_call(query, keys, values, head_dim)
    h_rows, u_rows = out_call(mixed, w_out, x_rows, moe_gain[None, :])
    acc = None
    first = 0
    for i, part in enumerate(expert_parts):
        acc = moe_call(u_rows, gates, part, acc, h_rows, first, i == len(expert_parts) - 1)
        first += part.shape[2]
    return acc


def solution(mesh):
    row_spec = P(('data', 'ep'))

    def device_step(x_in, w_query, w_keyval, w_out, attn_gain, moe_gain, w_gate, w_up, w_down, expert_ids, slot_ids, fill_counts, route_weight):
        batch_loc, seq_len, model_dim = x_in.shape
        rows_loc, num_heads, head_dim = w_query.shape
        q_cols = num_heads * head_dim
        k_cols = w_keyval.shape[1] // 2 * head_dim
        experts = w_gate.shape[0]
        choices = expert_ids.shape[-1]
        w_local = jnp.concatenate([w_query.reshape(rows_loc, q_cols), w_keyval.reshape(rows_loc, 2 * k_cols)], axis=1)
        w_qkv = lax.all_gather(w_local, 'ep', axis=0, tiled=True)
        per = experts // CHUNKS
        mats = (w_gate, w_up, jnp.swapaxes(w_down, 1, 2))
        stacks = [jnp.stack([mat[c * per:(c + 1) * per] for mat in mats]) for c in range(CHUNKS)]
        stacks, w_out, w_qkv = lax.optimization_barrier((stacks, w_out, w_qkv))
        full_out = lax.all_gather(w_out, 'ep', axis=0, tiled=True)
        expert_parts = [lax.all_gather(part, 'ep', axis=0, tiled=False) for part in stacks]
        outs = []
        for b in range(batch_loc):
            gates = gate_table(expert_ids[b], slot_ids[b], fill_counts[0], route_weight[b])
            outs.append(local_layer(x_in[b], w_qkv, full_out, attn_gain, moe_gain, expert_parts, gates, head_dim, q_cols, k_cols))
        return jnp.stack(outs)

    in_specs = (row_spec, P('ep'), P('ep'), P('ep'), P(), P(), P(None, 'ep'), P(None, 'ep'), P(None, None, 'ep'), row_spec, row_spec, row_spec, row_spec)
    return jax.shard_map(device_step, mesh=mesh, in_specs=in_specs, out_specs=row_spec, check_vma=False)
```

time: 3680 us -> 529 us (0.14)
  the two profiles are of different devices: /device:TPU:118 before, /device:TPU:97 now
where the time goes in v1:
time: 529 us; the launch traced here: 528 us
  Pallas kernels  450 us (85%)
  waiting for transfers between devices  42.5 us (8%)
  between operations  13.7 us (3%)
  other arithmetic  12.5 us (2%)
  local copies, waits for them, and re-layouts  8.93 us (2%)
    pallas_call x4, Pallas kernels, moe_call(): pl.pallas_call(functools.partial(moe_kernel, first_expert, is_first, is_l...  285 us
    pallas_call x1, Pallas kernels, attend_call(): pl.pallas_call(functools.partial(attend_kernel, head_dim), grid=(kv_heads...  138 us
    all_gather x1, waiting for transfers between devices, device_step(): w_qkv = lax.all_gather(w_local, 'ep', axis=0, tiled=True)  40 us
    pallas_call x1, Pallas kernels, qkv_call(): pl.pallas_call(functools.partial(qkv_kernel, head_dim, q_cols, k_cols), g...  15.9 us
    pallas_call x1, Pallas kernels, out_call(): pl.pallas_call(out_kernel, grid=(tokens // rows,), in_specs=[pl.BlockSpec...  11.9 us
  transfers between devices with their start and end apart: 6, of which 1 were waited for; matrix products, arithmetic and copies ran while one was open for 4% of the time, Pallas kernels for 72%

profile of v1, /device:TPU:97, one launch (start us, length us, event | category | flops | bytes accessed | tf_op | source)
XLA Modules:
  0.0 528.3 jit_solution(17719703565464031881)
XLA Ops:
  6.6 1.1 reshape.41
  7.7 1.0 reshape.42
  8.7 0.7 pad_maximum_fusion.5
  9.5 0.1 all-gather.13.cloned.1.call-start
  9.5 1.3 slice_bitcast_fusion.5
  10.8 1.3 slice_bitcast_fusion.4
  12.1 0.1 slice_bitcast_fusion
  12.1 1.3 pad_maximum_fusion.2
  13.5 1.3 pad_maximum_fusion
  14.8 40.0 %all-gather.11.cloned.1.call-done.w_ref = bf16[1024,2048]{1,0:T(8,128)(2,1)} async-done(((bf16[32,2048]{1,0:T(8,128)(2,1)}), bf16[1024,2048]{1,0:T(8,128)(2,1)}) %all-gather.11.cloned.1.call-update) | async-done | bytes 4194320 | tf_op jit(solution)/shard_map/all_gather | solution.py:362
  54.9 0.7 all-gather.21.cloned.1.call-update
  55.6 0.1 all-gather.19.cloned.1.call-start
  55.7 0.6 all-gather.19.cloned.1.call-update
  56.3 0.1 all-gather.17.cloned.1.call-start
  56.3 0.6 all-gather.17.cloned.1.call-update
  56.9 0.1 all-gather.15.cloned.1.call-start
  57.0 0.6 all-gather.15.cloned.1.call-update
  57.6 1.0 fusion.10
  58.7 0.1 tile.20
  58.8 1.3 copy.19.sin_ref
  60.1 0.1 tile.8
  60.2 1.3 copy.18.cos_ref
  61.5 0.6 broadcast_in_dim.95.gain_ref
  62.1 0.6 broadcast_in_dim.96.gain_ref
  62.9 8.1 %select_select_fusion.gate_ref = f32[2048,128]{1,0:T(8,128)} fusion(f32[2048]{0:T(1024)S(1)} %bitcast.68, s32[2048]{0:T(1024)S(1)} %bitcast.76, f32[2048]{0:T(1024)S(1)} %bitcast.69, s32[2048]{0:T(1024)S(1)} %bitcast.77, f32[2048]{0:T(1024)S(1)} %bitcast.70, s32[2048]{0:T(1024)S(1)} %bitcast.78, f32[2048]{0:T(1024)S(1)} %bitcast.71, s32[2048]{0:T(1024)S(1)} %bitcast.79, ...), kind=kLoop, calls=%fused_computation | loop fusion | flops 8388608 | bytes 1245696 | tf_op jit(solution)/shard_map/jit(_where)/select_n | solution.py:327
  71.0 15.9 %qkv_rope.1 = (bf16[2048,1024]{1,0:T(8,128)(2,1)}, bf16[2,2048,512]{2,1,0:T(8,128)(2,1)}, bf16[2,2048,512]{2,1,0:T(8,128)(2,1)}) custom-call(bf16[2048,1024]{1,0:T(8,128)(2,1)} %bitcast.95, bf16[1,1024]{1,0:T(2,128)(2,1)} %broadcast_in_dim.95.gain_ref, bf16[1024,2048]{1,0:T(8,128)(2,1)} %all-gather.11.cloned.1.call-done.w_ref, f32[2048,128]{1,0:T(8,128)} %copy.18.cos_ref, ...), custom_call_target="tpu_custom_call" | custom-call | flops 8589934592 | bytes 20971520 | tf_op jit(solution)/shard_map/qkv_rope/pallas_call | solution.py:71
  86.9 137.8 %attend.1.mixed_ref = bf16[2048,1024]{1,0:T(8,128)(2,1)} custom-call(bf16[2048,1024]{1,0:T(8,128)(2,1)} %get-tuple-element.17.q_ref, bf16[2,2048,512]{2,1,0:T(8,128)(2,1)} %get-tuple-element.18.ka_ref.kb_ref, bf16[2,2048,512]{2,1,0:T(8,128)(2,1)} %get-tuple-element.18.ka_ref.kb_ref, bf16[2,2048,512]{2,1,0:T(8,128)(2,1)} %get-tuple-element.19.va_ref.vb_ref, ...), custom_call_target="tpu_custom_call" | custom-call | flops 34359738368 | bytes 25165824 | tf_op jit(solution)/shard_map/attend/pallas_call | solution.py:179
  224.7 11.9 %out_proj.1 = (bf16[2048,1024]{1,0:T(8,128)(2,1)}, bf16[2048,1024]{1,0:T(8,128)(2,1)}) custom-call(bf16[2048,1024]{1,0:T(8,128)(2,1)} %attend.1.mixed_ref, bf16[1024,1024]{1,0:T(8,128)(2,1)} %all-gather.13.cloned.1.call-done.w_ref, bf16[2048,1024]{1,0:T(8,128)(2,1)} %bitcast.96, bf16[1,1024]{1,0:T(2,128)(2,1)} %broadcast_in_dim.96.gain_ref), custom_call_target="tpu_custom_call" | custom-call | flops 4294967296 | bytes 20971520 | tf_op jit(solution)/shard_map/out_proj/pallas_call | solution.py:213
  236.6 68.7 %moe_part.4.rest_0_ = f32[2048,1024]{1,0:T(8,128)} custom-call(bf16[2048,1024]{1,0:T(8,128)(2,1)} %get-tuple-element.21.u_ref, f32[2048,128]{1,0:T(8,128)} %select_select_fusion.gate_ref, bf16[32,3,8,32,512]{4,3,2,1,0:T(8,128)(2,1)} %bitcast.91), custom_call_target="tpu_custom_call" | custom-call | flops 51539607552 | bytes 58720256 | tf_op jit(solution)/shard_map/moe_part/pallas_call | solution.py:306
  305.3 71.8 %moe_part.5.rest_0_ = f32[2048,1024]{1,0:T(8,128)} custom-call(bf16[2048,1024]{1,0:T(8,128)(2,1)} %get-tuple-element.21.u_ref, f32[2048,128]{1,0:T(8,128)} %select_select_fusion.gate_ref, bf16[32,3,8,32,512]{4,3,2,1,0:T(8,128)(2,1)} %bitcast.92, f32[2048,1024]{1,0:T(8,128)} %moe_part.4.rest_0_), custom_call_target="tpu_custom_call", output_to_operand_aliasing={{}: (3, {})} | custom-call | flops 51539607552 | bytes 58720256 | tf_op jit(solution)/shard_map/moe_part/pallas_call | solution.py:306
  377.1 71.8 %moe_part.6.rest_0_ = f32[2048,1024]{1,0:T(8,128)} custom-call(bf16[2048,1024]{1,0:T(8,128)(2,1)} %get-tuple-element.21.u_ref, f32[2048,128]{1,0:T(8,128)} %select_select_fusion.gate_ref, bf16[32,3,8,32,512]{4,3,2,1,0:T(8,128)(2,1)} %bitcast.93, f32[2048,1024]{1,0:T(8,128)} %moe_part.5.rest_0_), custom_call_target="tpu_custom_call", output_to_operand_aliasing={{}: (3, {})} | custom-call | flops 51539607552 | bytes 58720256 | tf_op jit(solution)/shard_map/moe_part/pallas_call | solution.py:306
  448.9 72.5 %moe_part.7 = bf16[2048,1024]{1,0:T(8,128)(2,1)} custom-call(bf16[2048,1024]{1,0:T(8,128)(2,1)} %get-tuple-element.21.u_ref, f32[2048,128]{1,0:T(8,128)} %select_select_fusion.gate_ref, bf16[32,3,8,32,512]{4,3,2,1,0:T(8,128)(2,1)} %bitcast.94, f32[2048,1024]{1,0:T(8,128)} %moe_part.6.rest_0_, bf16[2048,1024]{1,0:T(8,128)(2,1)} %get-tuple-element.26.rest_1_), custom_call_target="tpu_custom_call" | custom-call | flops 51539607552 | bytes 58720256 | tf_op jit(solution)/shard_map/moe_part/pallas_call | solution.py:306
  (29 shorter events, 0.5 us)
Async XLA Ops:
  6.5 5.5 %copy-start = (bf16[32,512,32]{1,2,0:T(8,128)(2,1)S(1)}, bf16[32,512,32]{1,2,0:T(8,128)(2,1)}, u32[]{:S(2)}) copy-start(bf16[32,512,32]{1,2,0:T(8,128)(2,1)} %param.21) | copy-start | bytes 3145732
  6.5 48.2 %all-gather.11.cloned.1.call-start = ((), (), s32[]{:S(2)}) async-start(), calls=%async_computation | async-start | bytes 4325376 | tf_op jit(solution)/shard_map/all_gather | solution.py:362
  9.5 215.2 %all-gather.13.cloned.1.call-start = ((), (), s32[]{:S(2)}) async-start(), calls=%async_computation.1 | async-start | bytes 2162688 | tf_op jit(solution)/shard_map/all_gather | solution.py:367
  54.8 181.8 %all-gather.21.cloned.1.call-start = ((), (), s32[]{:S(2)}) async-start(), calls=%async_computation.5 | async-start | bytes 25952256 | tf_op jit(solution)/shard_map/all_gather | solution.py:368
  55.6 249.7 %all-gather.19.cloned.1.call-start = ((), (), s32[]{:S(2)}) async-start(), calls=%async_computation.4 | async-start | bytes 25952256 | tf_op jit(solution)/shard_map/all_gather | solution.py:368
  56.3 320.9 %all-gather.17.cloned.1.call-start = ((), (), s32[]{:S(2)}) async-start(), calls=%async_computation.3 | async-start | bytes 25952256 | tf_op jit(solution)/shard_map/all_gather | solution.py:368
  56.9 392.0 %all-gather.15.cloned.1.call-start = ((), (), s32[]{:S(2)}) async-start(), calls=%async_computation.2 | async-start | bytes 25952256 | tf_op jit(solution)/shard_map/all_gather | solution.py:368
  58.6 3.0 copy-start.4
  58.6 3.5 copy-start.5
  58.6 4.1 copy-start.6
  58.6 4.1 copy-start.1
  58.6 4.2 copy-start.2
  58.6 4.2 copy-start.3
Sparse Core Ops, SparseCore 0:
  9.6 45.1 all-gather.10
  56.8 37.6 all-gather.12
  96.6 85.8 all-gather.20
  184.5 86.0 all-gather.18
  272.5 86.0 all-gather.16
  360.5 86.0 all-gather.14

commit v2 on v1

--- a/solution.py
+++ b/solution.py
@@ -12,7 +12,8 @@
 ATT_ROWS = 512
 OUT_ROWS = 256
 MOE_ROWS = 512
-CHUNKS = 4
+MOE_PAIR = 2
+SHARES = (14, 11, 7)
 BIG_VMEM = 60 * 1024 * 1024
 
 
@@ -74,7 +75,7 @@
         in_specs=[
             pl.BlockSpec((rows, width), lambda i: (i, 0)),
             resident((1, width), lambda i: (0, 0)),
-            resident(w_qkv.shape, lambda i: (0, 0)),
+            resident((width, q_cols + 2 * k_cols), lambda i: (0, 0)),
             pl.BlockSpec((rows, LANES), lambda i: (i, 0)),
             pl.BlockSpec((rows, LANES), lambda i: (i, 0)),
         ],
@@ -89,83 +90,90 @@
             jax.ShapeDtypeStruct((2, tokens, k_cols), jnp.bfloat16),
         ],
         compiler_params=pltpu.CompilerParams(vmem_limit_bytes=BIG_VMEM),
-        cost_estimate=pl.CostEstimate(flops=2 * tokens * width * w_qkv.shape[1], bytes_accessed=tokens * width * 10, transcendentals=0),
+        cost_estimate=pl.CostEstimate(flops=2 * tokens * width * (q_cols + 2 * k_cols), bytes_accessed=tokens * width * 10, transcendentals=0),
         name='qkv_rope',
     )(x_rows, gain, w_qkv, cos_tab, sin_tab)
 
 
-def attend_kernel(head_dim, q_ref, ka_ref, kb_ref, va_ref, vb_ref, o_ref, s_buf, m_buf, l_buf, o_buf):
+def attend_kernel(head_dim, q_ref, ka_ref, kb_ref, va_ref, vb_ref, o_ref, q_buf, s_buf):
     rows = q_ref.shape[0]
+    half = rows // 2
+    tokens = ka_ref.shape[1]
     step = pl.program_id(1)
     lane = lax.broadcasted_iota(jnp.int32, (rows, LANES), 1)
     low = lane < head_dim
     query = q_ref[...].astype(jnp.float32) * (head_dim ** -0.5)
     zero = jnp.zeros_like(query)
-    heads = (jnp.where(low, query, zero).astype(jnp.bfloat16), jnp.where(low, zero, query).astype(jnp.bfloat16))
+    q_buf[0] = jnp.where(low, query, zero).astype(jnp.bfloat16)
+    q_buf[1] = jnp.where(low, zero, query).astype(jnp.bfloat16)
     key_refs = (ka_ref, kb_ref)
     val_refs = (va_ref, vb_ref)
-    groups = rows // LANES
-
-    def span(blk):
-        return pl.ds(pl.multiple_of(blk * rows, rows), rows)
-
-    def fold(op, tile):
-        out = tile[:, :LANES]
-        for g in range(1, groups):
-            out = op(out, tile[:, g * LANES:(g + 1) * LANES])
+
+    def fold(op, tile, out):
+        for g in range(tile.shape[1] // LANES):
+            part = tile[:, g * LANES:(g + 1) * LANES]
+            out = part if out is None else op(out, part)
         return out
 
-    def scores(head, blk, masked):
-        tile = f32dot_t(heads[head], key_refs[head][0, span(blk), :])
-        if masked:
-            row_id = lax.broadcasted_iota(jnp.int32, (rows, rows), 0)
-            col_id = lax.broadcasted_iota(jnp.int32, (rows, rows), 1)
-            tile = jnp.where(row_id >= col_id, tile, -1e30)
-        s_buf[head, :, span(blk)] = tile
-        m_buf[head] = jnp.maximum(m_buf[head], fold(jnp.maximum, tile))
-
-    def exps(head, blk, row_max):
-        tile = jnp.exp(s_buf[head, :, span(blk)] - row_max)
-        s_buf[head, :, span(blk)] = tile
-        l_buf[head] += fold(jnp.add, tile)
-
-    def mixes(head, blk, inv_sum):
-        prob = (s_buf[head, :, span(blk)] * inv_sum).astype(jnp.bfloat16)
-        o_buf[head] += f32dot(prob, val_refs[head][0, span(blk), :])
-
-    m_buf[...] = jnp.full_like(m_buf, -1e30)
-    l_buf[...] = jnp.zeros_like(l_buf)
-    o_buf[...] = jnp.zeros_like(o_buf)
-
-    @pl.loop(0, step)
-    def _(blk):
-        scores(0, blk, False)
-
-    scores(0, step, True)
-    max0 = jnp.max(m_buf[0], axis=-1, keepdims=True)
-
-    @pl.loop(0, step)
-    def _(blk):
-        scores(1, blk, False)
-        exps(0, blk, max0)
-
-    scores(1, step, True)
-    exps(0, step, max0)
-    max1 = jnp.max(m_buf[1], axis=-1, keepdims=True)
-    inv0 = 1.0 / jnp.sum(l_buf[0], axis=-1, keepdims=True)
-
-    @pl.loop(0, step + 1)
-    def _(blk):
-        mixes(0, blk, inv0)
-        exps(1, blk, max1)
-
-    inv1 = 1.0 / jnp.sum(l_buf[1], axis=-1, keepdims=True)
-
-    @pl.loop(0, step + 1)
-    def _(blk):
-        mixes(1, blk, inv1)
-
-    o_ref[...] = jnp.where(low, o_buf[0], o_buf[1]).astype(jnp.bfloat16)
+    def run_case(case):
+        chains = [dict(head=head, part=part, top=None, total=None, out=None) for part in range(2) for head in range(2)]
+        for chain in chains:
+            diag = (2 * case + chain['part']) * half
+            pieces = []
+            start = 0
+            while start < diag:
+                width = min(rows, diag - start)
+                pieces.append((start, width, False))
+                start += width
+            chain['pieces'] = pieces + [(diag, half, True)]
+
+        def scores(slot, chain, piece):
+            start, width, masked = piece
+            own = q_buf[chain['head'], chain['part'] * half:(chain['part'] + 1) * half, :]
+            tile = f32dot_t(own, key_refs[chain['head']][0, start:start + width, :])
+            if masked:
+                row_id = lax.broadcasted_iota(jnp.int32, (half, width), 0)
+                col_id = lax.broadcasted_iota(jnp.int32, (half, width), 1)
+                tile = jnp.where(row_id >= col_id, tile, -1e30)
+            s_buf[slot, :, start:start + width] = tile
+            chain['top'] = fold(jnp.maximum, tile, chain['top'])
+
+        def exps(slot, chain, piece):
+            start, width, _ = piece
+            tile = jnp.exp(s_buf[slot, :, start:start + width] - chain['row_max'])
+            s_buf[slot, :, start:start + width] = tile
+            chain['total'] = fold(jnp.add, tile, chain['total'])
+
+        def mixes(slot, chain, piece):
+            start, width, _ = piece
+            prob = (s_buf[slot, :, start:start + width] * chain['inv']).astype(jnp.bfloat16)
+            part = f32dot(prob, val_refs[chain['head']][0, start:start + width, :])
+            chain['out'] = part if chain['out'] is None else chain['out'] + part
+
+        count = len(chains)
+        for slot in range(count + 2):
+            work = []
+            if slot < count:
+                work.append((scores, slot))
+            if 0 <= slot - 1 < count:
+                chain = chains[slot - 1]
+                chain['row_max'] = jnp.max(chain['top'], axis=-1, keepdims=True)
+                work.append((exps, slot - 1))
+            if 0 <= slot - 2 < count:
+                chain = chains[slot - 2]
+                chain['inv'] = 1.0 / jnp.sum(chain['total'], axis=-1, keepdims=True)
+                work.append((mixes, slot - 2))
+            for j in range(max(len(chains[i]['pieces']) for _, i in work)):
+                for stage, i in work:
+                    if j < len(chains[i]['pieces']):
+                        stage(i, chains[i], chains[i]['pieces'][j])
+        low_half = low[:half]
+        for part in range(2):
+            first, second = chains[2 * part]['out'], chains[2 * part + 1]['out']
+            o_ref[part * half:(part + 1) * half, :] = jnp.where(low_half, first, second).astype(jnp.bfloat16)
+
+    for case in range(tokens // rows):
+        pl.when(step == case)(functools.partial(run_case, case))
 
 
 def attend_call(query, keys, values, head_dim):
@@ -189,10 +197,8 @@
         out_specs=pl.BlockSpec((rows, LANES), lambda h, i: (i, h)),
         out_shape=jax.ShapeDtypeStruct((tokens, q_cols), jnp.bfloat16),
         scratch_shapes=[
-            pltpu.VMEM((2, rows, tokens), jnp.float32),
-            pltpu.VMEM((2, rows, LANES), jnp.float32),
-            pltpu.VMEM((2, rows, LANES), jnp.float32),
-            pltpu.VMEM((2, rows, LANES), jnp.float32),
+            pltpu.VMEM((2, rows, LANES), jnp.bfloat16),
+            pltpu.VMEM((4, rows // 2, tokens), jnp.float32),
         ],
         compiler_params=pltpu.CompilerParams(vmem_limit_bytes=BIG_VMEM),
         cost_estimate=pl.CostEstimate(flops=8 * tokens * tokens * q_cols, bytes_accessed=tokens * q_cols * 12, transcendentals=tokens * tokens * q_cols // LANES),
@@ -206,7 +212,7 @@
     u_ref[...] = rms_rows(hidden.astype(jnp.float32), gain_ref[...].astype(jnp.float32))
 
 
-def out_call(mixed, w_out, x_rows, gain):
+def out_call(mixed, w_attn, x_rows, gain):
     tokens, width = x_rows.shape
     rows = OUT_ROWS
     block = pl.BlockSpec((rows, width), lambda i: (i, 0))
@@ -215,7 +221,7 @@
         grid=(tokens // rows,),
         in_specs=[
             pl.BlockSpec((rows, mixed.shape[1]), lambda i: (i, 0)),
-            resident(w_out.shape, lambda i: (0, 0)),
+            resident((mixed.shape[1], width), lambda i: (0, w_attn.shape[1] // width - 1)),
             block,
             resident((1, width), lambda i: (0, 0)),
         ],
@@ -224,7 +230,7 @@
         compiler_params=pltpu.CompilerParams(vmem_limit_bytes=BIG_VMEM),
         cost_estimate=pl.CostEstimate(flops=2 * tokens * width * mixed.shape[1], bytes_accessed=tokens * width * 10, transcendentals=0),
         name='out_proj',
-    )(mixed, w_out, x_rows, gain)
+    )(mixed, w_attn, x_rows, gain)
 
 
 def moe_kernel(first_expert, is_first, is_last, u_ref, gate_ref, w_ref, *rest):
@@ -249,21 +255,26 @@
             copy.start()
             copy.wait()
 
-    w_gate = w_ref[:, 0, 0].reshape(full, inner)
-    w_up = w_ref[:, 1, 0].reshape(full, inner)
-    w_down = w_ref[:, 2, 0].reshape(full, inner)
     tokens = u_ref.shape[0]
 
-    @pl.loop(0, tokens // MOE_ROWS)
-    def _(blk):
-        rows = pl.ds(pl.multiple_of(blk * MOE_ROWS, MOE_ROWS), MOE_ROWS)
-        in_rows = u_ref[rows, :]
-        hidden_mid = (jax.nn.silu(f32dot(in_rows, w_gate)) * f32dot(in_rows, w_up)).astype(jnp.bfloat16)
-        y_rows = f32dot_t(hidden_mid, w_down).astype(jnp.bfloat16).astype(jnp.float32)
-        gates = gate_ref[rows, :]
-        lane = lax.broadcasted_iota(jnp.int32, gates.shape, 1)
-        weight = jnp.sum(jnp.where(lane == expert, gates, 0.0), axis=-1, keepdims=True)
-        acc[rows, :] += jnp.where(weight > 0, weight * y_rows, 0.0)
+    @pl.loop(0, tokens // (MOE_PAIR * MOE_ROWS))
+    def _(trip):
+        def span(i):
+            return pl.ds(pl.multiple_of((trip * MOE_PAIR + i) * MOE_ROWS, MOE_ROWS), MOE_ROWS)
+
+        def matrix(i):
+            return w_ref[:, i, 0].reshape(full, inner)
+
+        mids = []
+        for i in range(MOE_PAIR):
+            in_rows = u_ref[span(i), :]
+            mids.append((jax.nn.silu(f32dot(in_rows, matrix(0))) * f32dot(in_rows, matrix(1))).astype(jnp.bfloat16))
+        for i in range(MOE_PAIR):
+            y_rows = f32dot_t(mids[i], matrix(2)).astype(jnp.bfloat16).astype(jnp.float32)
+            gates = gate_ref[span(i), :]
+            lane = lax.broadcasted_iota(jnp.int32, gates.shape, 1)
+            weight = jnp.sum(jnp.where(lane == expert, gates, 0.0), axis=-1, keepdims=True)
+            acc[span(i), :] += jnp.where(weight > 0, weight * y_rows, 0.0)
 
     @pl.when(step == pl.num_programs(0) - 1)
     def _():
@@ -328,18 +339,19 @@
     return table
 
 
-def local_layer(x_rows, w_qkv, w_out, attn_gain, moe_gain, expert_parts, gates, head_dim, q_cols, k_cols):
-    tokens, width = x_rows.shape
+def rotary_tables(tokens, head_dim):
     half_dim = head_dim // 2
     inv_freq = 10000.0 ** (-jnp.arange(half_dim, dtype=jnp.float32) / half_dim)
     angles = jnp.arange(tokens, dtype=jnp.float32)[:, None] * inv_freq[None, :]
     cos_half, sin_half = jnp.cos(angles), jnp.sin(angles)
     reps = LANES // head_dim
-    cos_tab = jnp.tile(cos_half, (1, 2 * reps))
-    sin_tab = jnp.tile(jnp.concatenate([-sin_half, sin_half], axis=1), (1, reps))
-    query, keys, values = qkv_call(x_rows, attn_gain[None, :], w_qkv, cos_tab, sin_tab, head_dim, q_cols, k_cols)
+    return jnp.tile(cos_half, (1, 2 * reps)), jnp.tile(jnp.concatenate([-sin_half, sin_half], axis=1), (1, reps))
+
+
+def local_layer(x_rows, w_attn, attn_gain, moe_gain, expert_parts, gates, tables, head_dim, q_cols, k_cols):
+    query, keys, values = qkv_call(x_rows, attn_gain, w_attn, *tables, head_dim, q_cols, k_cols)
     mixed = attend_call(query, keys, values, head_dim)
-    h_rows, u_rows = out_call(mixed, w_out, x_rows, moe_gain[None, :])
+    h_rows, u_rows = out_call(mixed, w_attn, x_rows, moe_gain)
     acc = None
     first = 0
     for i, part in enumerate(expert_parts):
@@ -348,6 +360,12 @@
     return acc
 
 
+def shares_of(experts):
+    total = sum(SHARES)
+    sizes = [experts * share // total for share in SHARES[1:]]
+    return [experts - sum(sizes)] + sizes
+
+
 def solution(mesh):
     row_spec = P(('data', 'ep'))
 
@@ -357,19 +375,22 @@
         q_cols = num_heads * head_dim
         k_cols = w_keyval.shape[1] // 2 * head_dim
         experts = w_gate.shape[0]
-        choices = expert_ids.shape[-1]
-        w_local = jnp.concatenate([w_query.reshape(rows_loc, q_cols), w_keyval.reshape(rows_loc, 2 * k_cols)], axis=1)
-        w_qkv = lax.all_gather(w_local, 'ep', axis=0, tiled=True)
-        per = experts // CHUNKS
+        w_local = jnp.concatenate([w_query.reshape(rows_loc, q_cols), w_keyval.reshape(rows_loc, 2 * k_cols), w_out], axis=1)
+        w_attn = lax.all_gather(w_local, 'ep', axis=0, tiled=True)
         mats = (w_gate, w_up, jnp.swapaxes(w_down, 1, 2))
-        stacks = [jnp.stack([mat[c * per:(c + 1) * per] for mat in mats]) for c in range(CHUNKS)]
-        stacks, w_out, w_qkv = lax.optimization_barrier((stacks, w_out, w_qkv))
-        full_out = lax.all_gather(w_out, 'ep', axis=0, tiled=True)
+        stacks = []
+        first = 0
+        for size in shares_of(experts):
+            stacks.append(jnp.stack([mat[first:first + size] for mat in mats]))
+            first += size
+        tables = rotary_tables(seq_len, head_dim)
+        gates = [gate_table(expert_ids[b], slot_ids[b], fill_counts[0], route_weight[b]) for b in range(batch_loc)]
+        gains = (attn_gain[None, :], moe_gain[None, :])
+        stacks, tables, gates, gains, w_attn = lax.optimization_barrier((stacks, tables, gates, gains, w_attn))
         expert_parts = [lax.all_gather(part, 'ep', axis=0, tiled=False) for part in stacks]
         outs = []
         for b in range(batch_loc):
-            gates = gate_table(expert_ids[b], slot_ids[b], fill_counts[0], route_weight[b])
-            outs.append(local_layer(x_in[b], w_qkv, full_out, attn_gain, moe_gain, expert_parts, gates, head_dim, q_cols, k_cols))
+            outs.append(local_layer(x_in[b], w_attn, *gains, expert_parts, gates[b], tables, head_dim, q_cols, k_cols))
         return jnp.stack(outs)
 
     in_specs = (row_spec, P('ep'), P('ep'), P('ep'), P(), P(), P(None, 'ep'), P(None, 'ep'), P(None, None, 'ep'), row_spec, row_spec, row_spec, row_spec)

time: 529 us -> 463 us (0.88)
  Pallas kernels: 450 us -> 356 us
  waiting for transfers between devices: 42.5 us -> 66.6 us
    pallas_call x1, Pallas kernels: 138 us -> 74.1 us  [attend_call(): pl.pallas_call(functools.partial(attend_kernel, head_dim), grid=(kv_heads...]
    all_gather x4 -> x3, waiting for transfers between devices: 0.06 us -> 37.3 us  [device_step(): lax.all_gather(part, 'ep', axis=0, tiled=False)]
    pallas_call x4 -> x3, Pallas kernels: 285 us -> 254 us  [moe_call(): pl.pallas_call(functools.partial(moe_kernel, first_expert, is_first, is_l...]
    all_gather x2 -> x1, waiting for transfers between devices: 40 us -> 28.2 us  [device_step(): w_attn = lax.all_gather(w_local, 'ep', axis=0, tiled=True)]
  transfers between devices with their start and end apart: 6 -> 4, of which waited for: 1 -> 3; matrix products, arithmetic and copies ran while one was open for 4% -> 5% of each run, Pallas kernels for 72% -> 64%
where the time goes in v2:
time: 463 us
  Pallas kernels  356 us (77%)
  waiting for transfers between devices  66.6 us (14%)
  other arithmetic  13.8 us (3%)
  between operations  13.3 us (3%)
  local copies, waits for them, and re-layouts  12.6 us (3%)
    pallas_call x3, Pallas kernels, moe_call(): pl.pallas_call(functools.partial(moe_kernel, first_expert, is_first, is_l...  254 us
    pallas_call x1, Pallas kernels, attend_call(): pl.pallas_call(functools.partial(attend_kernel, head_dim), grid=(kv_heads...  74.1 us
    all_gather x3, waiting for transfers between devices, device_step(): lax.all_gather(part, 'ep', axis=0, tiled=False)  37.3 us
    all_gather x1, waiting for transfers between devices, device_step(): w_attn = lax.all_gather(w_local, 'ep', axis=0, tiled=True)  28.2 us
    pallas_call x1, Pallas kernels, qkv_call(): pl.pallas_call(functools.partial(qkv_kernel, head_dim, q_cols, k_cols), g...  15.8 us
    pallas_call x1, Pallas kernels, out_call(): pl.pallas_call(out_kernel, grid=(tokens // rows,), in_specs=[pl.BlockSpec...  11.9 us
  transfers between devices with their start and end apart: 4, of which 3 were waited for; matrix products, arithmetic and copies ran while one was open for 5% of the time, Pallas kernels for 64%

profile of v2, /device:TPU:97, one launch (start us, length us, event | category | flops | bytes accessed | tf_op | source)
XLA Modules:
  0.0 462.5 jit_solution(17789518123814715941)
XLA Ops:
  6.6 1.2 reshape.41
  7.7 1.0 reshape.42
  8.8 1.5 pad_maximum_fusion.4
  10.4 0.1 all-gather.14.cloned.1.call-start
  10.5 1.3 broadcast_in_dim.120.gain_ref
  11.7 1.3 broadcast_in_dim.121.gain_ref
  13.0 0.7 pad.4
  13.7 1.0 slice_bitcast_fusion.8
  14.6 1.1 slice_bitcast_fusion.6
  15.7 0.9 pad_maximum_fusion.2
  16.7 1.0 slice_bitcast_fusion.5
  17.8 1.1 pad_maximum_fusion.1
  18.9 1.1 slice_bitcast_fusion.2
  20.0 1.2 pad_maximum_fusion
  21.3 1.0 fusion.10
  22.5 7.9 %select_select_fusion.gate_ref = f32[2048,128]{1,0:T(8,128)} fusion(f32[2048]{0:T(1024)S(1)} %bitcast.63, s32[2048]{0:T(1024)S(1)} %bitcast.71, f32[2048]{0:T(1024)S(1)} %bitcast.64, s32[2048]{0:T(1024)S(1)} %bitcast.72, f32[2048]{0:T(1024)S(1)} %bitcast.65, s32[2048]{0:T(1024)S(1)} %bitcast.73, f32[2048]{0:T(1024)S(1)} %bitcast.66, s32[2048]{0:T(1024)S(1)} %bitcast.74, ...), kind=kLoop, calls=%fused_computation.2 | loop fusion | flops 8388608 | bytes 1245696 | tf_op jit(solution)/shard_map/jit(_where)/select_n | solution.py:338
  30.4 28.2 %all-gather.8.cloned.1.call-done.w_ref = bf16[1024,3072]{1,0:T(8,128)(2,1)} async-done(((bf16[32,3072]{1,0:T(8,128)(2,1)}), bf16[1024,3072]{1,0:T(8,128)(2,1)}) %all-gather.8.cloned.1.call-update) | async-done | bytes 6291472 | tf_op jit(solution)/shard_map/all_gather | solution.py:379
  58.6 0.1 tile.20
  58.7 0.1 tile.8
  59.0 0.7 all-gather.12.cloned.1.call-update
  59.7 0.2 all-gather.10.cloned.1.call-start
  59.9 0.4 all-gather.10.cloned.1.call-update
  60.3 1.3 copy.17.cos_ref
  61.6 1.3 copy.18.sin_ref
  63.0 15.8 %qkv_rope.1 = (bf16[2048,1024]{1,0:T(8,128)(2,1)}, bf16[2,2048,512]{2,1,0:T(8,128)(2,1)}, bf16[2,2048,512]{2,1,0:T(8,128)(2,1)}) custom-call(bf16[2048,1024]{1,0:T(8,128)(2,1)} %bitcast.89, bf16[1,1024]{1,0:T(2,128)(2,1)} %broadcast_in_dim.120.gain_ref, bf16[1024,3072]{1,0:T(8,128)(2,1)} %all-gather.8.cloned.1.call-done.w_ref, f32[2048,128]{1,0:T(8,128)} %copy.17.cos_ref, ...), custom_call_target="tpu_custom_call" | custom-call | flops 8589934592 | bytes 20971520 | tf_op jit(solution)/shard_map/qkv_rope/pallas_call | solution.py:72
  78.7 74.1 %attend.1.mixed_ref = bf16[2048,1024]{1,0:T(8,128)(2,1)} custom-call(bf16[2048,1024]{1,0:T(8,128)(2,1)} %get-tuple-element.23.q_ref, bf16[2,2048,512]{2,1,0:T(8,128)(2,1)} %get-tuple-element.24.ka_ref.kb_ref, bf16[2,2048,512]{2,1,0:T(8,128)(2,1)} %get-tuple-element.24.ka_ref.kb_ref, bf16[2,2048,512]{2,1,0:T(8,128)(2,1)} %get-tuple-element.25.va_ref.vb_ref, ...), custom_call_target="tpu_custom_call" | custom-call | flops 34359738368 | bytes 25165824 | tf_op jit(solution)/shard_map/attend/pallas_call | solution.py:187
  152.8 11.9 %out_proj.1 = (bf16[2048,1024]{1,0:T(8,128)(2,1)}, bf16[2048,1024]{1,0:T(8,128)(2,1)}) custom-call(bf16[2048,1024]{1,0:T(8,128)(2,1)} %attend.1.mixed_ref, bf16[1024,3072]{1,0:T(8,128)(2,1)} %all-gather.8.cloned.1.call-done.w_ref, bf16[2048,1024]{1,0:T(8,128)(2,1)} %bitcast.90, bf16[1,1024]{1,0:T(2,128)(2,1)} %broadcast_in_dim.121.gain_ref), custom_call_target="tpu_custom_call" | custom-call | flops 4294967296 | bytes 20971520 | tf_op jit(solution)/shard_map/out_proj/pallas_call | solution.py:219
  164.7 30.6 %all-gather.14.cloned.1.call-done = bf16[96,14,32,512]{3,2,1,0:T(8,128)(2,1)} async-done(((bf16[3,14,32,512]{3,2,1,0:T(8,128)(2,1)}), bf16[96,14,32,512]{3,2,1,0:T(8,128)(2,1)}) %all-gather.14.cloned.1.call-update) | async-done | bytes 44040208 | tf_op jit(solution)/shard_map/all_gather | solution.py:390
  195.3 105.9 %moe_part.3.rest_0_ = f32[2048,1024]{1,0:T(8,128)} custom-call(bf16[2048,1024]{1,0:T(8,128)(2,1)} %get-tuple-element.27.u_ref, f32[2048,128]{1,0:T(8,128)} %select_select_fusion.gate_ref, bf16[32,3,14,32,512]{4,3,2,1,0:T(8,128)(2,1)} %bitcast.86), custom_call_target="tpu_custom_call" | custom-call | flops 90194313216 | bytes 77594624 | tf_op jit(solution)/shard_map/moe_part/pallas_call | solution.py:317
  301.2 6.6 %all-gather.12.cloned.1.call-done = bf16[96,11,32,512]{3,2,1,0:T(8,128)(2,1)} async-done(((bf16[3,11,32,512]{3,2,1,0:T(8,128)(2,1)}), bf16[96,11,32,512]{3,2,1,0:T(8,128)(2,1)}) %all-gather.12.cloned.1.call-update) | async-done | bytes 34603024 | tf_op jit(solution)/shard_map/all_gather | solution.py:390
  307.8 87.8 %moe_part.4.rest_0_ = f32[2048,1024]{1,0:T(8,128)} custom-call(bf16[2048,1024]{1,0:T(8,128)(2,1)} %get-tuple-element.27.u_ref, f32[2048,128]{1,0:T(8,128)} %select_select_fusion.gate_ref, bf16[32,3,11,32,512]{4,3,2,1,0:T(8,128)(2,1)} %bitcast.87, f32[2048,1024]{1,0:T(8,128)} %moe_part.3.rest_0_), custom_call_target="tpu_custom_call", output_to_operand_aliasing={{}: (3, {})} | custom-call | flops 70866960384 | bytes 68157440 | tf_op jit(solution)/shard_map/moe_part/pallas_call | solution.py:317
  395.6 60.3 %moe_part.5 = bf16[2048,1024]{1,0:T(8,128)(2,1)} custom-call(bf16[2048,1024]{1,0:T(8,128)(2,1)} %get-tuple-element.27.u_ref, f32[2048,128]{1,0:T(8,128)} %select_select_fusion.gate_ref, bf16[32,3,7,32,512]{4,3,2,1,0:T(8,128)(2,1)} %bitcast.88, f32[2048,1024]{1,0:T(8,128)} %moe_part.4.rest_0_, bf16[2048,1024]{1,0:T(8,128)(2,1)} %get-tuple-element.32.rest_1_), custom_call_target="tpu_custom_call" | custom-call | flops 45097156608 | bytes 55574528 | tf_op jit(solution)/shard_map/moe_part/pallas_call | solution.py:317
  (22 shorter events, 0.5 us)
Async XLA Ops:
  6.5 11.1 %copy-start = (bf16[32,512,32]{1,2,0:T(8,128)(2,1)S(1)}, bf16[32,512,32]{1,2,0:T(8,128)(2,1)}, u32[]{:S(2)}) copy-start(bf16[32,512,32]{1,2,0:T(8,128)(2,1)} %param.21) | copy-start | bytes 3145732
  6.5 11.1 %copy-start.1 = (bf16[32,32,512]{2,1,0:T(8,128)(2,1)S(1)}, bf16[32,32,512]{2,1,0:T(8,128)(2,1)}, u32[]{:S(2)}) copy-start(bf16[32,32,512]{2,1,0:T(8,128)(2,1)} %param.20) | copy-start | bytes 3145732
  6.6 52.1 %all-gather.8.cloned.1.call-start = ((), (), s32[]{:S(2)}) async-start(), calls=%async_computation | async-start | bytes 6488064 | tf_op jit(solution)/shard_map/all_gather | solution.py:379
  10.4 184.9 %all-gather.14.cloned.1.call-start = ((), (), s32[]{:S(2)}) async-start(), calls=%async_computation.3 | async-start | bytes 45416448 | tf_op jit(solution)/shard_map/all_gather | solution.py:390
  18.9 3.4 copy-start.2
  18.9 3.5 copy-start.3
  18.9 3.6 copy-start.4
  58.9 248.9 %all-gather.12.cloned.1.call-start = ((), (), s32[]{:S(2)}) async-start(), calls=%async_computation.2 | async-start | bytes 35684352 | tf_op jit(solution)/shard_map/all_gather | solution.py:390
  59.7 335.9 %all-gather.10.cloned.1.call-start = ((), (), s32[]{:S(2)}) async-start(), calls=%async_computation.1 | async-start | bytes 22708224 | tf_op jit(solution)/shard_map/all_gather | solution.py:390
Sparse Core Ops, SparseCore 0:
  10.5 48.0 all-gather.7
  60.7 134.5 all-gather.13
  197.4 110.3 all-gather.11
  309.7 78.6 all-gather.9

commit v3 on v2

--- a/solution.py
+++ b/solution.py
@@ -13,7 +13,8 @@
 OUT_ROWS = 256
 MOE_ROWS = 512
 MOE_PAIR = 2
-SHARES = (14, 11, 7)
+FEW_ROWS = 256
+SHARES = (16, 10, 6)
 BIG_VMEM = 60 * 1024 * 1024
 
 
@@ -233,79 +234,109 @@
     )(mixed, w_attn, x_rows, gain)
 
 
-def moe_kernel(first_expert, is_first, is_last, u_ref, gate_ref, w_ref, *rest):
-    if is_first:
-        rest = (None,) + rest
-    acc_in, *rest = rest
-    if is_last:
-        h_ref, out_ref, acc, sem = rest
-    else:
-        out_ref, acc, sem = rest
+def moe_kernel(first_expert, is_first, is_last, count_ref, u_ref, gate_ref, slot_ref, slot_row_ref, w_ref, *rest):
+    rest = list(rest)
+    acc_in = None if is_first else rest.pop(0)
+    h_ref = rest.pop(0) if is_last else None
+    out_ref, acc, prior, sems = rest
     step = pl.program_id(0)
     expert = first_expert + step
     shards, _, _, depth, inner = w_ref.shape
     full = shards * depth
+    tokens = u_ref.shape[0]
+    count = count_ref[expert]
+
+    def span(blk):
+        return pl.ds(pl.multiple_of(blk * MOE_ROWS, MOE_ROWS), MOE_ROWS)
+
+    def matrix(i):
+        return w_ref[:, i, 0].reshape(full, inner)
+
+    def column(ref, rows):
+        vals = ref[rows, :]
+        lane = lax.broadcasted_iota(jnp.int32, vals.shape, 1)
+        return jnp.sum(jnp.where(lane == expert, vals, jnp.zeros_like(vals)), axis=-1, keepdims=True)
+
+    def middle(in_rows):
+        return (jax.nn.silu(f32dot(in_rows, matrix(0))) * f32dot(in_rows, matrix(1))).astype(jnp.bfloat16)
 
     @pl.when(step == 0)
     def _():
-        if is_first:
-            acc[...] = jnp.zeros_like(acc)
-        else:
-            copy = pltpu.make_async_copy(acc_in, acc, sem)
-            copy.start()
-            copy.wait()
-
-    tokens = u_ref.shape[0]
-
-    @pl.loop(0, tokens // (MOE_PAIR * MOE_ROWS))
-    def _(trip):
-        def span(i):
-            return pl.ds(pl.multiple_of((trip * MOE_PAIR + i) * MOE_ROWS, MOE_ROWS), MOE_ROWS)
-
-        def matrix(i):
-            return w_ref[:, i, 0].reshape(full, inner)
-
-        mids = []
-        for i in range(MOE_PAIR):
-            in_rows = u_ref[span(i), :]
-            mids.append((jax.nn.silu(f32dot(in_rows, matrix(0))) * f32dot(in_rows, matrix(1))).astype(jnp.bfloat16))
-        for i in range(MOE_PAIR):
-            y_rows = f32dot_t(mids[i], matrix(2)).astype(jnp.bfloat16).astype(jnp.float32)
-            gates = gate_ref[span(i), :]
-            lane = lax.broadcasted_iota(jnp.int32, gates.shape, 1)
-            weight = jnp.sum(jnp.where(lane == expert, gates, 0.0), axis=-1, keepdims=True)
-            acc[span(i), :] += jnp.where(weight > 0, weight * y_rows, 0.0)
+        if not is_first:
+            pltpu.make_async_copy(acc_in, prior, sems.at[0]).start()
+
+        @pl.loop(0, tokens // MOE_ROWS)
+        def _(blk):
+            acc[span(blk), :] = jnp.zeros((MOE_ROWS, acc.shape[1]), jnp.float32)
+
+    @pl.when(count > FEW_ROWS)
+    def _():
+        @pl.loop(0, tokens // (MOE_PAIR * MOE_ROWS))
+        def _(trip):
+            spans = [span(trip * MOE_PAIR + i) for i in range(MOE_PAIR)]
+            mids = [middle(u_ref[rows, :]) for rows in spans]
+            for rows, mid in zip(spans, mids):
+                y_rows = f32dot_t(mid, matrix(2)).astype(jnp.bfloat16).astype(jnp.float32)
+                weight = column(gate_ref, rows)
+                acc[rows, :] += jnp.where(weight > 0, weight * y_rows, 0.0)
+
+    @pl.when((count > 0) & (count <= FEW_ROWS))
+    def _():
+        place = lax.broadcasted_iota(jnp.int32, (FEW_ROWS, tokens), 0)
+        pick = jnp.where(slot_row_ref[pl.ds(expert, 1), :] == place, 1.0, 0.0).astype(jnp.bfloat16)
+        in_rows = f32dot(pick, u_ref[...]).astype(jnp.bfloat16)
+        y_rows = f32dot_t(middle(in_rows), matrix(2)).astype(jnp.bfloat16)
+
+        @pl.loop(0, tokens // MOE_ROWS)
+        def _(blk):
+            rows = span(blk)
+            place = lax.broadcasted_iota(jnp.int32, (MOE_ROWS, FEW_ROWS), 1).astype(jnp.float32)
+            spread = jnp.where(column(slot_ref, rows) == place, column(gate_ref, rows), 0.0).astype(jnp.bfloat16)
+            acc[rows, :] += f32dot(spread, y_rows)
 
     @pl.when(step == pl.num_programs(0) - 1)
     def _():
-        if is_last:
+        if not is_first:
+            pltpu.make_async_copy(acc_in, prior, sems.at[0]).wait()
+
+        def out_copy(blk):
+            return pltpu.make_async_copy(acc.at[span(blk), :], out_ref.at[span(blk), :], sems.at[1])
+
+        @pl.loop(0, tokens // MOE_ROWS)
+        def _(blk):
+            rows = span(blk)
+            total = acc[rows, :] if is_first else acc[rows, :] + prior[rows, :]
+            if is_last:
+                out_ref[rows, :] = (h_ref[rows, :].astype(jnp.float32) + total).astype(jnp.bfloat16)
+            else:
+                if not is_first:
+                    acc[rows, :] = total
+                out_copy(blk).start()
+
+        if not is_last:
             @pl.loop(0, tokens // MOE_ROWS)
             def _(blk):
-                rows = pl.ds(pl.multiple_of(blk * MOE_ROWS, MOE_ROWS), MOE_ROWS)
-                out_ref[rows, :] = (h_ref[rows, :].astype(jnp.float32) + acc[rows, :]).astype(jnp.bfloat16)
-        else:
-            copy = pltpu.make_async_copy(acc, out_ref, sem)
-            copy.start()
-            copy.wait()
-
-
-def moe_call(u_rows, gates, weights, acc, h_rows, first_expert, is_last):
+                out_copy(blk).wait()
+
+
+def moe_call(u_rows, routing, weights, acc, h_rows, first_expert, is_last):
     tokens, width = u_rows.shape
     shards, parts, count, depth, inner = weights.shape
     is_first = acc is None
     whole = lambda e: (0, 0)
-    args = [u_rows, gates, weights]
+    counts, gates, slots, slot_rows = routing
+    args = [counts, u_rows, gates, slots, slot_rows, weights]
     in_specs = [
+        pl.BlockSpec(memory_space=pltpu.SMEM),
         resident((tokens, width), whole),
         resident(gates.shape, whole),
+        resident(slots.shape, whole),
+        resident(slot_rows.shape, whole),
         pl.BlockSpec((shards, parts, 1, depth, inner), lambda e: (0, 0, e, 0, 0)),
     ]
-    aliases = {}
     if not is_first:
         args.append(acc)
         in_specs.append(pl.BlockSpec(memory_space=pl.ANY))
-        if not is_last:
-            aliases = {3: 0}
     if is_last:
         args.append(h_rows)
         in_specs.append(resident((tokens, width), whole))
@@ -314,48 +345,55 @@
     else:
         out_spec = pl.BlockSpec(memory_space=pl.ANY)
         out_shape = jax.ShapeDtypeStruct((tokens, width), jnp.float32)
+    prior_shape = (8, LANES) if is_first else (tokens, width)
     return pl.pallas_call(
         functools.partial(moe_kernel, first_expert, is_first, is_last),
         grid=(count,),
         in_specs=in_specs,
         out_specs=out_spec,
         out_shape=out_shape,
-        scratch_shapes=[pltpu.VMEM((tokens, width), jnp.float32), pltpu.SemaphoreType.DMA],
-        input_output_aliases=aliases,
+        scratch_shapes=[pltpu.VMEM((tokens, width), jnp.float32), pltpu.VMEM(prior_shape, jnp.float32), pltpu.SemaphoreType.DMA((2,))],
         compiler_params=pltpu.CompilerParams(vmem_limit_bytes=BIG_VMEM),
         cost_estimate=pl.CostEstimate(flops=6 * tokens * width * inner * count, bytes_accessed=2 * weights.size + 16 * tokens * width, transcendentals=tokens * inner * count),
         name='moe_part',
     )(*args)
 
 
-def gate_table(expert_ids, slot_ids, counts, weights):
+def routing_tables(expert_ids, slot_ids, counts, weights):
     tokens, choices = expert_ids.shape
-    limits = jnp.pad(counts, (0, LANES - counts.shape[0]))[None, :]
+    experts = counts.shape[0]
+    limits = jnp.pad(counts, (0, LANES - experts))[None, :]
     lane = lax.broadcasted_iota(jnp.int32, (tokens, LANES), 1)
-    table = jnp.zeros((tokens, LANES), jnp.float32)
+    row = lax.broadcasted_iota(jnp.int32, (experts, tokens), 0)
+    gates = jnp.zeros((tokens, LANES), jnp.float32)
+    slots = jnp.full((tokens, LANES), -1.0, jnp.float32)
+    slot_rows = jnp.full((experts, tokens), -1, jnp.int32)
     for k in range(choices):
-        kept = (expert_ids[:, k:k + 1] == lane) & (slot_ids[:, k:k + 1] < limits)
-        table = jnp.where(kept, weights[:, k:k + 1].astype(jnp.float32), table)
-    return table
+        ids, slot = expert_ids[:, k], slot_ids[:, k]
+        kept = (ids[:, None] == lane) & (slot[:, None] < limits)
+        gates = jnp.where(kept, weights[:, k:k + 1].astype(jnp.float32), gates)
+        slots = jnp.where(kept, slot[:, None].astype(jnp.float32), slots)
+        slot_rows = jnp.where((ids[None, :] == row) & (slot[None, :] < counts[:, None]), slot[None, :], slot_rows)
+    return counts, gates, slots, slot_rows
 
 
 def rotary_tables(tokens, head_dim):
     half_dim = head_dim // 2
-    inv_freq = 10000.0 ** (-jnp.arange(half_dim, dtype=jnp.float32) / half_dim)
+    lane = jnp.arange(LANES)
+    inv_freq = 10000.0 ** (-(lane % half_dim).astype(jnp.float32) / half_dim)
     angles = jnp.arange(tokens, dtype=jnp.float32)[:, None] * inv_freq[None, :]
-    cos_half, sin_half = jnp.cos(angles), jnp.sin(angles)
-    reps = LANES // head_dim
-    return jnp.tile(cos_half, (1, 2 * reps)), jnp.tile(jnp.concatenate([-sin_half, sin_half], axis=1), (1, reps))
-
-
-def local_layer(x_rows, w_attn, attn_gain, moe_gain, expert_parts, gates, tables, head_dim, q_cols, k_cols):
+    sign = jnp.where(lane % head_dim < half_dim, -1.0, 1.0)
+    return jnp.cos(angles), jnp.sin(angles) * sign[None, :]
+
+
+def local_layer(x_rows, w_attn, attn_gain, moe_gain, expert_parts, routing, tables, head_dim, q_cols, k_cols):
     query, keys, values = qkv_call(x_rows, attn_gain, w_attn, *tables, head_dim, q_cols, k_cols)
     mixed = attend_call(query, keys, values, head_dim)
     h_rows, u_rows = out_call(mixed, w_attn, x_rows, moe_gain)
     acc = None
     first = 0
     for i, part in enumerate(expert_parts):
-        acc = moe_call(u_rows, gates, part, acc, h_rows, first, i == len(expert_parts) - 1)
+        acc = moe_call(u_rows, routing, part, acc, h_rows, first, i == len(expert_parts) - 1)
         first += part.shape[2]
     return acc
 
@@ -384,13 +422,13 @@
             stacks.append(jnp.stack([mat[first:first + size] for mat in mats]))
             first += size
         tables = rotary_tables(seq_len, head_dim)
-        gates = [gate_table(expert_ids[b], slot_ids[b], fill_counts[0], route_weight[b]) for b in range(batch_loc)]
+        routing = [routing_tables(expert_ids[b], slot_ids[b], fill_counts[0], route_weight[b]) for b in range(batch_loc)]
         gains = (attn_gain[None, :], moe_gain[None, :])
-        stacks, tables, gates, gains, w_attn = lax.optimization_barrier((stacks, tables, gates, gains, w_attn))
+        stacks, tables, routing, gains, w_attn = lax.optimization_barrier((stacks, tables, routing, gains, w_attn))
         expert_parts = [lax.all_gather(part, 'ep', axis=0, tiled=False) for part in stacks]
         outs = []
         for b in range(batch_loc):
-            outs.append(local_layer(x_in[b], w_attn, *gains, expert_parts, gates[b], tables, head_dim, q_cols, k_cols))
+            outs.append(local_layer(x_in[b], w_attn, *gains, expert_parts, routing[b], tables, head_dim, q_cols, k_cols))
         return jnp.stack(outs)
 
     in_specs = (row_spec, P('ep'), P('ep'), P('ep'), P(), P(), P(None, 'ep'), P(None, 'ep'), P(None, None, 'ep'), row_spec, row_spec, row_spec, row_spec)

time: 463 us -> 444 us (0.959)
  Pallas kernels: 356 us -> 323 us
  other arithmetic: 13.8 us -> 26.6 us
  waiting for transfers between devices: 66.6 us -> 71.4 us
    pallas_call x3, Pallas kernels: 254 us -> 222 us  [moe_call(): pl.pallas_call(functools.partial(moe_kernel, first_expert, is_first, is_l...]
    all_gather x3, waiting for transfers between devices: 37.3 us -> 53.7 us  [device_step(): lax.all_gather(part, 'ep', axis=0, tiled=False)]
    all_gather x1, waiting for transfers between devices: 28.2 us -> 16.5 us  [device_step(): w_attn = lax.all_gather(w_local, 'ep', axis=0, tiled=True)]
    select_n x1 -> x4, other arithmetic: 7.92 us -> 16.8 us  [the longest x1 7.88 us: routing_tables(): slots = jnp.where(kept, slot[:, None].astype(jnp.float32), slots)]
    mul x0 -> x1, other arithmetic: none -> 4.79 us  [rotary_tables(): return (jnp.cos(angles), jnp.sin(angles) * sign[None, :])]
  transfers between devices with their start and end apart: 4 -> 4, of which waited for: 3 -> 4; matrix products, arithmetic and copies ran while one was open for 5% -> 7% of each run, Pallas kernels for 64% -> 62%
where the time goes in v3:
time: 444 us
  Pallas kernels  323 us (73%)
  waiting for transfers between devices  71.4 us (16%)
  other arithmetic  26.6 us (6%)
  between operations  13.3 us (3%)
  local copies, waits for them, and re-layouts  8.69 us (2%)
    pallas_call x3, Pallas kernels, moe_call(): pl.pallas_call(functools.partial(moe_kernel, first_expert, is_first, is_l...  222 us
    pallas_call x1, Pallas kernels, attend_call(): pl.pallas_call(functools.partial(attend_kernel, head_dim), grid=(kv_heads...  74.1 us
    all_gather x3, waiting for transfers between devices, device_step(): lax.all_gather(part, 'ep', axis=0, tiled=False)  53.7 us
    all_gather x1, waiting for transfers between devices, device_step(): w_attn = lax.all_gather(w_local, 'ep', axis=0, tiled=True)  16.5 us
    pallas_call x1, Pallas kernels, qkv_call(): pl.pallas_call(functools.partial(qkv_kernel, head_dim, q_cols, k_cols), g...  15.8 us
    pallas_call x1, Pallas kernels, out_call(): pl.pallas_call(out_kernel, grid=(tokens // rows,), in_specs=[pl.BlockSpec...  11.9 us
  transfers between devices with their start and end apart: 4, of which 4 were waited for; matrix products, arithmetic and copies ran while one was open for 7% of the time, Pallas kernels for 62%

profile of v3, /device:TPU:97, one launch (start us, length us, event | category | flops | bytes accessed | tf_op | source)
XLA Modules:
  0.0 443.9 jit_solution(15302279332650781744)
XLA Ops:
  6.6 1.2 reshape.48
  7.8 1.0 reshape.49
  8.8 1.5 pad_maximum_fusion.3
  10.4 0.1 all-gather.14.cloned.1.call-start
  10.5 1.3 broadcast_in_dim.238.gain_ref
  11.7 1.3 broadcast_in_dim.239.gain_ref
  13.0 0.7 pad.4
  13.7 0.9 slice_bitcast_fusion.8
  14.6 1.1 slice_bitcast_fusion.6
  15.7 0.9 pad_maximum_fusion.2
  16.6 1.0 slice_bitcast_fusion.5
  17.7 1.1 pad_maximum_fusion.1
  18.9 0.1 slice_bitcast_fusion
  18.9 1.3 pad_maximum_fusion
  20.4 0.1 slice_convert_fusion.15
  20.5 1.1 select_select_fusion.2.slot_row_ref
  21.5 7.9 %select_select_fusion.slot_ref = f32[2048,128]{1,0:T(8,128)} fusion(f32[2048]{0:T(1024)S(1)} %bitcast.129, f32[2048]{0:T(1024)S(1)} %bitcast.128, f32[2048]{0:T(1024)S(1)} %bitcast.127, f32[2048]{0:T(1024)S(1)} %bitcast.126, f32[2048]{0:T(1024)S(1)} %bitcast.125, f32[2048]{0:T(1024)S(1)} %bitcast.124, f32[2048]{0:T(1024)S(1)} %bitcast.123, ...), kind=kLoop, calls=%fused_computation.1 | loop fusion | flops 8388608 | bytes 1245696 | tf_op jit(solution)/shard_map/jit(_where)/select_n | solution.py:375
  29.4 7.9 %select_select_fusion.1.gate_ref = f32[2048,128]{1,0:T(8,128)} fusion(f32[2048]{0:T(1024)S(1)} %bitcast.115, s32[2048]{0:T(1024)S(1)} %bitcast.68, f32[2048]{0:T(1024)S(1)} %bitcast.116, s32[2048]{0:T(1024)S(1)} %bitcast.71, f32[2048]{0:T(1024)S(1)} %bitcast.117, s32[2048]{0:T(1024)S(1)} %bitcast.74, f32[2048]{0:T(1024)S(1)} %bitcast.118, ...), kind=kLoop, calls=%fused_computation.2 | loop fusion | flops 8388608 | bytes 1245696 | tf_op jit(solution)/shard_map/jit(_where)/select_n | solution.py:374
  37.3 4.8 %sine_multiply_fusion = (f32[2048,128]{1,0:T(8,128)}, f32[2048,128]{1,0:T(8,128)}) fusion(f32[128]{0:T(128)S(1)} %get-tuple-element.79, f32[128]{0:T(128)S(1)} %get-tuple-element.80), kind=kLoop, calls=%fused_computation.11 | loop fusion | flops 524288 | bytes 2098176 | tf_op jit(solution)/shard_map/mul | solution.py:386
  42.1 16.5 %all-gather.8.cloned.1.call-done.w_ref = bf16[1024,3072]{1,0:T(8,128)(2,1)} async-done(((bf16[32,3072]{1,0:T(8,128)(2,1)}), bf16[1024,3072]{1,0:T(8,128)(2,1)}) %all-gather.8.cloned.1.call-update) | async-done | bytes 6291472 | tf_op jit(solution)/shard_map/all_gather | solution.py:417
  58.7 0.7 all-gather.12.cloned.1.call-update
  59.5 0.2 all-gather.10.cloned.1.call-start
  59.7 0.4 all-gather.10.cloned.1.call-update
  60.1 15.8 %qkv_rope.1 = (bf16[2048,1024]{1,0:T(8,128)(2,1)}, bf16[2,2048,512]{2,1,0:T(8,128)(2,1)}, bf16[2,2048,512]{2,1,0:T(8,128)(2,1)}) custom-call(bf16[2048,1024]{1,0:T(8,128)(2,1)} %bitcast.138, bf16[1,1024]{1,0:T(2,128)(2,1)} %broadcast_in_dim.238.gain_ref, bf16[1024,3072]{1,0:T(8,128)(2,1)} %all-gather.8.cloned.1.call-done.w_ref, ...), custom_call_target="tpu_custom_call" | custom-call | flops 8589934592 | bytes 20971520 | tf_op jit(solution)/shard_map/qkv_rope/pallas_call | solution.py:73
  75.9 74.1 %attend.1.mixed_ref = bf16[2048,1024]{1,0:T(8,128)(2,1)} custom-call(bf16[2048,1024]{1,0:T(8,128)(2,1)} %get-tuple-element.27.q_ref, bf16[2,2048,512]{2,1,0:T(8,128)(2,1)} %get-tuple-element.28.ka_ref.kb_ref, bf16[2,2048,512]{2,1,0:T(8,128)(2,1)} %get-tuple-element.28.ka_ref.kb_ref, bf16[2,2048,512]{2,1,0:T(8,128)(2,1)} %get-tuple-element.29.va_ref.vb_ref, ...), custom_call_target="tpu_custom_call" | custom-call | flops 34359738368 | bytes 25165824 | tf_op jit(solution)/shard_map/attend/pallas_call | solution.py:188
  150.0 11.9 %out_proj.1 = (bf16[2048,1024]{1,0:T(8,128)(2,1)}, bf16[2048,1024]{1,0:T(8,128)(2,1)}) custom-call(bf16[2048,1024]{1,0:T(8,128)(2,1)} %attend.1.mixed_ref, bf16[1024,3072]{1,0:T(8,128)(2,1)} %all-gather.8.cloned.1.call-done.w_ref, bf16[2048,1024]{1,0:T(8,128)(2,1)} %bitcast.139, bf16[1,1024]{1,0:T(2,128)(2,1)} %broadcast_in_dim.239.gain_ref), custom_call_target="tpu_custom_call" | custom-call | flops 4294967296 | bytes 20971520 | tf_op jit(solution)/shard_map/out_proj/pallas_call | solution.py:220
  161.9 49.8 %all-gather.14.cloned.1.call-done = bf16[96,16,32,512]{3,2,1,0:T(8,128)(2,1)} async-done(((bf16[3,16,32,512]{3,2,1,0:T(8,128)(2,1)}), bf16[96,16,32,512]{3,2,1,0:T(8,128)(2,1)}) %all-gather.14.cloned.1.call-update) | async-done | bytes 50331664 | tf_op jit(solution)/shard_map/all_gather | solution.py:428
  211.7 103.6 %moe_part.3.rest_0_ = f32[2048,1024]{1,0:T(8,128)} custom-call(s32[32]{0:T(128)} %bitcast.131, bf16[2048,1024]{1,0:T(8,128)(2,1)} %get-tuple-element.31.u_ref, f32[2048,128]{1,0:T(8,128)} %select_select_fusion.1.gate_ref, f32[2048,128]{1,0:T(8,128)} %select_select_fusion.slot_ref, s32[32,2048]{1,0:T(8,128)} %select_select_fusion.2.slot_row_ref, ...), custom_call_target="tpu_custom_call" | custom-call | flops 103079215104 | bytes 83886080 | tf_op jit(solution)/shard_map/moe_part/pallas_call | solution.py:349
  315.3 0.3 all-gather.12.cloned.1.call-done
  315.6 69.9 %moe_part.4.rest_0_ = f32[2048,1024]{1,0:T(8,128)} custom-call(s32[32]{0:T(128)} %bitcast.132, bf16[2048,1024]{1,0:T(8,128)(2,1)} %get-tuple-element.31.u_ref, f32[2048,128]{1,0:T(8,128)} %select_select_fusion.1.gate_ref, f32[2048,128]{1,0:T(8,128)} %select_select_fusion.slot_ref, s32[32,2048]{1,0:T(8,128)} %select_select_fusion.2.slot_row_ref, ...), custom_call_target="tpu_custom_call" | custom-call | flops 64424509440 | bytes 65011712 | tf_op jit(solution)/shard_map/moe_part/pallas_call | solution.py:349
  385.5 3.6 all-gather.10.cloned.1.call-done
  389.1 48.2 %moe_part.5 = bf16[2048,1024]{1,0:T(8,128)(2,1)} custom-call(s32[32]{0:T(128)} %bitcast.133, bf16[2048,1024]{1,0:T(8,128)(2,1)} %get-tuple-element.31.u_ref, f32[2048,128]{1,0:T(8,128)} %select_select_fusion.1.gate_ref, f32[2048,128]{1,0:T(8,128)} %select_select_fusion.slot_ref, s32[32,2048]{1,0:T(8,128)} %select_select_fusion.2.slot_row_ref, ...), custom_call_target="tpu_custom_call" | custom-call | flops 38654705664 | bytes 52428800 | tf_op jit(solution)/shard_map/moe_part/pallas_call | solution.py:349
  (23 shorter events, 0.4 us)
Async XLA Ops:
  6.5 12.3 %copy-start = (bf16[32,32,512]{2,1,0:T(8,128)(2,1)S(1)}, bf16[32,32,512]{2,1,0:T(8,128)(2,1)}, u32[]{:S(2)}) copy-start(bf16[32,32,512]{2,1,0:T(8,128)(2,1)} %param.19) | copy-start | bytes 3145732
  6.5 11.0 %copy-start.1 = (bf16[32,512,32]{1,2,0:T(8,128)(2,1)S(1)}, bf16[32,512,32]{1,2,0:T(8,128)(2,1)}, u32[]{:S(2)}) copy-start(bf16[32,512,32]{1,2,0:T(8,128)(2,1)} %param.21) | copy-start | bytes 3145732
  6.6 11.1 %copy-start.2 = (bf16[32,32,512]{2,1,0:T(8,128)(2,1)S(1)}, bf16[32,32,512]{2,1,0:T(8,128)(2,1)}, u32[]{:S(2)}) copy-start(bf16[32,32,512]{2,1,0:T(8,128)(2,1)} %param.20) | copy-start | bytes 3145732
  6.6 52.1 %all-gather.8.cloned.1.call-start = ((), (), s32[]{:S(2)}) async-start(), calls=%async_computation | async-start | bytes 6488064 | tf_op jit(solution)/shard_map/all_gather | solution.py:417
  10.4 201.3 %all-gather.14.cloned.1.call-start = ((), (), s32[]{:S(2)}) async-start(), calls=%async_computation.3 | async-start | bytes 51904512 | tf_op jit(solution)/shard_map/all_gather | solution.py:428
  17.7 2.6 copy-start.3
  17.7 2.6 copy-start.5
  17.7 2.7 copy-start.4
  17.7 2.8 copy-start.6
  58.7 256.9 %all-gather.12.cloned.1.call-start = ((), (), s32[]{:S(2)}) async-start(), calls=%async_computation.2 | async-start | bytes 32440320 | tf_op jit(solution)/shard_map/all_gather | solution.py:428
  59.5 329.6 %all-gather.10.cloned.1.call-start = ((), (), s32[]{:S(2)}) async-start(), calls=%async_computation.1 | async-start | bytes 19464192 | tf_op jit(solution)/shard_map/all_gather | solution.py:428
Sparse Core Ops, SparseCore 0:
  10.5 48.0 all-gather.7
  60.7 150.9 all-gather.13
  213.7 101.8 all-gather.11
  317.5 71.4 all-gather.9

commit v4 on v3

--- a/solution.py
+++ b/solution.py
@@ -14,7 +14,10 @@
 MOE_ROWS = 512
 MOE_PAIR = 2
 FEW_ROWS = 256
-SHARES = (16, 10, 6)
+SPREAD_ROWS = 256
+PASS_ROWS = 64
+MATRICES = 3
+SHARES = (4, 14, 9, 5)
 BIG_VMEM = 60 * 1024 * 1024
 
 
@@ -49,26 +52,34 @@
         other = jnp.where(low_half, pltpu.roll(v32, LANES - half_dim, 1), pltpu.roll(v32, half_dim, 1))
         return v32 * cos_tab + other * sin_tab
 
-    query = f32dot(normed, w_ref[:, :q_cols])
-    for c in range(q_cols // LANES):
-        cols = slice(c * LANES, (c + 1) * LANES)
-        q_ref[:, cols] = rotated(query[:, cols]).astype(jnp.bfloat16)
-    keys = f32dot(normed, w_ref[:, q_cols:q_cols + k_cols])
-    for c in range(k_cols // LANES):
-        cols = slice(c * LANES, (c + 1) * LANES)
-        rot = rotated(keys[:, cols]).astype(jnp.bfloat16).astype(jnp.float32)
-        kk_ref[0, :, cols] = rot.astype(jnp.bfloat16)
-        kk_ref[1, :, cols] = pltpu.roll(rot, head_dim, 1).astype(jnp.bfloat16)
-    values = f32dot(normed, w_ref[:, q_cols + k_cols:])
-    for c in range(k_cols // LANES):
-        cols = slice(c * LANES, (c + 1) * LANES)
-        val = values[:, cols].astype(jnp.bfloat16).astype(jnp.float32)
-        vv_ref[0, :, cols] = val.astype(jnp.bfloat16)
-        vv_ref[1, :, cols] = pltpu.roll(val, head_dim, 1).astype(jnp.bfloat16)
-
-
-def qkv_call(x_rows, gain, w_qkv, cos_tab, sin_tab, head_dim, q_cols, k_cols):
+    shards, _, depth, inner = w_ref.shape
+
+    def product(block):
+        return f32dot(normed, w_ref[:, block].reshape(shards * depth, inner))
+
+    chunks = inner // LANES
+    for block in range(q_cols // inner):
+        query = product(block)
+        for c in range(chunks):
+            cols = slice(block * inner + c * LANES, block * inner + (c + 1) * LANES)
+            q_ref[:, cols] = rotated(query[:, c * LANES:(c + 1) * LANES]).astype(jnp.bfloat16)
+    for block in range(k_cols // inner):
+        keys = product(q_cols // inner + block)
+        values = product((q_cols + k_cols) // inner + block)
+        for c in range(chunks):
+            own = slice(c * LANES, (c + 1) * LANES)
+            cols = slice(block * inner + c * LANES, block * inner + (c + 1) * LANES)
+            rot = rotated(keys[:, own]).astype(jnp.bfloat16).astype(jnp.float32)
+            kk_ref[0, :, cols] = rot.astype(jnp.bfloat16)
+            kk_ref[1, :, cols] = pltpu.roll(rot, head_dim, 1).astype(jnp.bfloat16)
+            val = values[:, own].astype(jnp.bfloat16).astype(jnp.float32)
+            vv_ref[0, :, cols] = val.astype(jnp.bfloat16)
+            vv_ref[1, :, cols] = pltpu.roll(val, head_dim, 1).astype(jnp.bfloat16)
+
+
+def qkv_call(x_rows, gain, blocks, cos_tab, sin_tab, head_dim, q_cols, k_cols):
     tokens, width = x_rows.shape
+    shards, _, depth, inner = blocks.shape
     rows = QKV_ROWS
     return pl.pallas_call(
         functools.partial(qkv_kernel, head_dim, q_cols, k_cols),
@@ -76,7 +87,7 @@
         in_specs=[
             pl.BlockSpec((rows, width), lambda i: (i, 0)),
             resident((1, width), lambda i: (0, 0)),
-            resident((width, q_cols + 2 * k_cols), lambda i: (0, 0)),
+            resident((shards, (q_cols + 2 * k_cols) // inner, depth, inner), lambda i: (0, 0, 0, 0)),
             pl.BlockSpec((rows, LANES), lambda i: (i, 0)),
             pl.BlockSpec((rows, LANES), lambda i: (i, 0)),
         ],
@@ -93,7 +104,7 @@
         compiler_params=pltpu.CompilerParams(vmem_limit_bytes=BIG_VMEM),
         cost_estimate=pl.CostEstimate(flops=2 * tokens * width * (q_cols + 2 * k_cols), bytes_accessed=tokens * width * 10, transcendentals=0),
         name='qkv_rope',
-    )(x_rows, gain, w_qkv, cos_tab, sin_tab)
+    )(x_rows, gain, blocks, cos_tab, sin_tab)
 
 
 def attend_kernel(head_dim, q_ref, ka_ref, kb_ref, va_ref, vb_ref, o_ref, q_buf, s_buf):
@@ -208,13 +219,18 @@
 
 
 def out_kernel(mixed_ref, w_ref, x_ref, gain_ref, h_ref, u_ref):
-    hidden = (x_ref[...].astype(jnp.float32) + f32dot(mixed_ref[...], w_ref[...])).astype(jnp.bfloat16)
+    shards, parts, depth, inner = w_ref.shape
+    mixed = mixed_ref[...]
+    attn_out = jnp.concatenate([f32dot(mixed, w_ref[:, i].reshape(shards * depth, inner)) for i in range(parts)], axis=1)
+    hidden = (x_ref[...].astype(jnp.float32) + attn_out).astype(jnp.bfloat16)
     h_ref[...] = hidden
     u_ref[...] = rms_rows(hidden.astype(jnp.float32), gain_ref[...].astype(jnp.float32))
 
 
-def out_call(mixed, w_attn, x_rows, gain):
+def out_call(mixed, blocks, first_block, x_rows, gain):
     tokens, width = x_rows.shape
+    shards, _, depth, inner = blocks.shape
+    parts = width // inner
     rows = OUT_ROWS
     block = pl.BlockSpec((rows, width), lambda i: (i, 0))
     return pl.pallas_call(
@@ -222,7 +238,7 @@
         grid=(tokens // rows,),
         in_specs=[
             pl.BlockSpec((rows, mixed.shape[1]), lambda i: (i, 0)),
-            resident((mixed.shape[1], width), lambda i: (0, w_attn.shape[1] // width - 1)),
+            resident((shards, parts, depth, inner), lambda i: (0, first_block // parts, 0, 0)),
             block,
             resident((1, width), lambda i: (0, 0)),
         ],
@@ -231,26 +247,32 @@
         compiler_params=pltpu.CompilerParams(vmem_limit_bytes=BIG_VMEM),
         cost_estimate=pl.CostEstimate(flops=2 * tokens * width * mixed.shape[1], bytes_accessed=tokens * width * 10, transcendentals=0),
         name='out_proj',
-    )(mixed, w_attn, x_rows, gain)
-
-
-def moe_kernel(first_expert, is_first, is_last, count_ref, u_ref, gate_ref, slot_ref, slot_row_ref, w_ref, *rest):
+    )(mixed, blocks, x_rows, gain)
+
+
+def moe_kernel(first_expert, is_first, is_last, count_ref, u_ref, gate_ref, slot_ref, slot_row_ref, w1_ref, w3_ref, w2_ref, *rest):
     rest = list(rest)
     acc_in = None if is_first else rest.pop(0)
     h_ref = rest.pop(0) if is_last else None
     out_ref, acc, prior, sems = rest
     step = pl.program_id(0)
     expert = first_expert + step
-    shards, _, _, depth, inner = w_ref.shape
+    shards, _, depth, inner = w1_ref.shape
     full = shards * depth
+    mat_refs = (w1_ref, w3_ref, w2_ref)
+    pair = 1 if is_first else MOE_PAIR
+    few = 0 if is_first else FEW_ROWS
     tokens = u_ref.shape[0]
     count = count_ref[expert]
 
     def span(blk):
         return pl.ds(pl.multiple_of(blk * MOE_ROWS, MOE_ROWS), MOE_ROWS)
 
+    def strip(blk):
+        return pl.ds(pl.multiple_of(blk * PASS_ROWS, PASS_ROWS), PASS_ROWS)
+
     def matrix(i):
-        return w_ref[:, i, 0].reshape(full, inner)
+        return mat_refs[i][:, 0].reshape(full, inner)
 
     def column(ref, rows):
         vals = ref[rows, :]
@@ -265,34 +287,36 @@
         if not is_first:
             pltpu.make_async_copy(acc_in, prior, sems.at[0]).start()
 
-        @pl.loop(0, tokens // MOE_ROWS)
+        @pl.loop(0, tokens // PASS_ROWS)
         def _(blk):
-            acc[span(blk), :] = jnp.zeros((MOE_ROWS, acc.shape[1]), jnp.float32)
-
-    @pl.when(count > FEW_ROWS)
+            acc[strip(blk), :] = jnp.zeros((PASS_ROWS, acc.shape[1]), jnp.float32)
+
+    @pl.when(count > few)
     def _():
-        @pl.loop(0, tokens // (MOE_PAIR * MOE_ROWS))
+        @pl.loop(0, tokens // (pair * MOE_ROWS))
         def _(trip):
-            spans = [span(trip * MOE_PAIR + i) for i in range(MOE_PAIR)]
+            spans = [span(trip * pair + i) for i in range(pair)]
             mids = [middle(u_ref[rows, :]) for rows in spans]
             for rows, mid in zip(spans, mids):
                 y_rows = f32dot_t(mid, matrix(2)).astype(jnp.bfloat16).astype(jnp.float32)
                 weight = column(gate_ref, rows)
                 acc[rows, :] += jnp.where(weight > 0, weight * y_rows, 0.0)
 
-    @pl.when((count > 0) & (count <= FEW_ROWS))
-    def _():
-        place = lax.broadcasted_iota(jnp.int32, (FEW_ROWS, tokens), 0)
+    def few_step():
+        place = lax.broadcasted_iota(jnp.int32, (few, tokens), 0)
         pick = jnp.where(slot_row_ref[pl.ds(expert, 1), :] == place, 1.0, 0.0).astype(jnp.bfloat16)
         in_rows = f32dot(pick, u_ref[...]).astype(jnp.bfloat16)
         y_rows = f32dot_t(middle(in_rows), matrix(2)).astype(jnp.bfloat16)
 
-        @pl.loop(0, tokens // MOE_ROWS)
+        @pl.loop(0, tokens // SPREAD_ROWS)
         def _(blk):
-            rows = span(blk)
-            place = lax.broadcasted_iota(jnp.int32, (MOE_ROWS, FEW_ROWS), 1).astype(jnp.float32)
+            rows = pl.ds(pl.multiple_of(blk * SPREAD_ROWS, SPREAD_ROWS), SPREAD_ROWS)
+            place = lax.broadcasted_iota(jnp.int32, (SPREAD_ROWS, few), 1).astype(jnp.float32)
             spread = jnp.where(column(slot_ref, rows) == place, column(gate_ref, rows), 0.0).astype(jnp.bfloat16)
             acc[rows, :] += f32dot(spread, y_rows)
+
+    if few:
+        pl.when((count > 0) & (count <= few))(few_step)
 
     @pl.when(step == pl.num_programs(0) - 1)
     def _():
@@ -300,11 +324,11 @@
             pltpu.make_async_copy(acc_in, prior, sems.at[0]).wait()
 
         def out_copy(blk):
-            return pltpu.make_async_copy(acc.at[span(blk), :], out_ref.at[span(blk), :], sems.at[1])
-
-        @pl.loop(0, tokens // MOE_ROWS)
+            return pltpu.make_async_copy(acc.at[strip(blk), :], out_ref.at[strip(blk), :], sems.at[1])
+
+        @pl.loop(0, tokens // PASS_ROWS)
         def _(blk):
-            rows = span(blk)
+            rows = strip(blk)
             total = acc[rows, :] if is_first else acc[rows, :] + prior[rows, :]
             if is_last:
                 out_ref[rows, :] = (h_ref[rows, :].astype(jnp.float32) + total).astype(jnp.bfloat16)
@@ -314,26 +338,28 @@
                 out_copy(blk).start()
 
         if not is_last:
-            @pl.loop(0, tokens // MOE_ROWS)
+            @pl.loop(0, tokens // PASS_ROWS)
             def _(blk):
                 out_copy(blk).wait()
 
 
-def moe_call(u_rows, routing, weights, acc, h_rows, first_expert, is_last):
+def moe_call(u_rows, routing, blocks, first_block, acc, h_rows, first_expert, is_last):
     tokens, width = u_rows.shape
-    shards, parts, count, depth, inner = weights.shape
+    shards, total, depth, inner = blocks.shape
+    count = (total - first_block) // MATRICES
     is_first = acc is None
     whole = lambda e: (0, 0)
     counts, gates, slots, slot_rows = routing
-    args = [counts, u_rows, gates, slots, slot_rows, weights]
+    args = [counts, u_rows, gates, slots, slot_rows, blocks, blocks, blocks]
     in_specs = [
         pl.BlockSpec(memory_space=pltpu.SMEM),
         resident((tokens, width), whole),
         resident(gates.shape, whole),
         resident(slots.shape, whole),
         resident(slot_rows.shape, whole),
-        pl.BlockSpec((shards, parts, 1, depth, inner), lambda e: (0, 0, e, 0, 0)),
     ]
+    for i in range(MATRICES):
+        in_specs.append(pl.BlockSpec((shards, 1, depth, inner), lambda e, i=i: (0, first_block + i * count + e, 0, 0)))
     if not is_first:
         args.append(acc)
         in_specs.append(pl.BlockSpec(memory_space=pl.ANY))
@@ -354,7 +380,7 @@
         out_shape=out_shape,
         scratch_shapes=[pltpu.VMEM((tokens, width), jnp.float32), pltpu.VMEM(prior_shape, jnp.float32), pltpu.SemaphoreType.DMA((2,))],
         compiler_params=pltpu.CompilerParams(vmem_limit_bytes=BIG_VMEM),
-        cost_estimate=pl.CostEstimate(flops=6 * tokens * width * inner * count, bytes_accessed=2 * weights.size + 16 * tokens * width, transcendentals=tokens * inner * count),
+        cost_estimate=pl.CostEstimate(flops=6 * tokens * width * inner * count, bytes_accessed=2 * blocks.size + 16 * tokens * width, transcendentals=tokens * inner * count),
         name='moe_part',
     )(*args)
 
@@ -386,15 +412,17 @@
     return jnp.cos(angles), jnp.sin(angles) * sign[None, :]
 
 
-def local_layer(x_rows, w_attn, attn_gain, moe_gain, expert_parts, routing, tables, head_dim, q_cols, k_cols):
-    query, keys, values = qkv_call(x_rows, attn_gain, w_attn, *tables, head_dim, q_cols, k_cols)
+def local_layer(x_rows, attn_gain, moe_gain, parts, attn_blocks, routing, tables, head_dim, q_cols, k_cols):
+    query, keys, values = qkv_call(x_rows, attn_gain, parts[0], *tables, head_dim, q_cols, k_cols)
     mixed = attend_call(query, keys, values, head_dim)
-    h_rows, u_rows = out_call(mixed, w_attn, x_rows, moe_gain)
+    inner = parts[0].shape[-1]
+    h_rows, u_rows = out_call(mixed, parts[0], (q_cols + 2 * k_cols) // inner, x_rows, moe_gain)
     acc = None
-    first = 0
-    for i, part in enumerate(expert_parts):
-        acc = moe_call(u_rows, routing, part, acc, h_rows, first, i == len(expert_parts) - 1)
-        first += part.shape[2]
+    expert = 0
+    for i, blocks in enumerate(parts):
+        first_block = 0 if i else attn_blocks
+        acc = moe_call(u_rows, routing, blocks, first_block, acc, h_rows, expert, i == len(parts) - 1)
+        expert += (blocks.shape[1] - first_block) // MATRICES
     return acc
 
 
@@ -413,22 +441,26 @@
         q_cols = num_heads * head_dim
         k_cols = w_keyval.shape[1] // 2 * head_dim
         experts = w_gate.shape[0]
+        inner = w_gate.shape[2]
         w_local = jnp.concatenate([w_query.reshape(rows_loc, q_cols), w_keyval.reshape(rows_loc, 2 * k_cols), w_out], axis=1)
-        w_attn = lax.all_gather(w_local, 'ep', axis=0, tiled=True)
+        attn_blocks = w_local.shape[1] // inner
         mats = (w_gate, w_up, jnp.swapaxes(w_down, 1, 2))
         stacks = []
         first = 0
         for size in shares_of(experts):
-            stacks.append(jnp.stack([mat[first:first + size] for mat in mats]))
+            stacks.append([mat[first:first + size] for mat in mats])
             first += size
+        stacks[0] = [w_local[None, :, i * inner:(i + 1) * inner] for i in range(attn_blocks)] + stacks[0]
+        stacks = [jnp.concatenate(stack) for stack in stacks]
+        head = lax.all_gather(stacks[0], 'ep', axis=0, tiled=False)
         tables = rotary_tables(seq_len, head_dim)
         routing = [routing_tables(expert_ids[b], slot_ids[b], fill_counts[0], route_weight[b]) for b in range(batch_loc)]
         gains = (attn_gain[None, :], moe_gain[None, :])
-        stacks, tables, routing, gains, w_attn = lax.optimization_barrier((stacks, tables, routing, gains, w_attn))
-        expert_parts = [lax.all_gather(part, 'ep', axis=0, tiled=False) for part in stacks]
+        stacks, tables, routing, gains, head = lax.optimization_barrier((stacks[1:], tables, routing, gains, head))
+        parts = [head] + [lax.all_gather(part, 'ep', axis=0, tiled=False) for part in stacks]
         outs = []
         for b in range(batch_loc):
-            outs.append(local_layer(x_in[b], w_attn, *gains, expert_parts, routing[b], tables, head_dim, q_cols, k_cols))
+            outs.append(local_layer(x_in[b], *gains, parts, attn_blocks, routing[b], tables, head_dim, q_cols, k_cols))
         return jnp.stack(outs)
 
     in_specs = (row_spec, P('ep'), P('ep'), P('ep'), P(), P(), P(None, 'ep'), P(None, 'ep'), P(None, None, 'ep'), row_spec, row_spec, row_spec, row_spec)

time: 444 us -> 446 us (level)
  Pallas kernels: 323 us -> 347 us
  waiting for transfers between devices: 71.4 us -> 48.6 us
    all_gather x3, waiting for transfers between devices: 53.7 us -> 0.06 us  [device_step(): lax.all_gather(part, 'ep', axis=0, tiled=False)]
    all_gather x1, waiting for transfers between devices: 16.5 us -> 47.3 us  [device_step(): head = lax.all_gather(stacks[0], 'ep', axis=0, tiled=False)]
    pallas_call x3 -> x4, Pallas kernels: 222 us -> 245 us  [moe_call(): pl.pallas_call(functools.partial(moe_kernel, first_expert, is_first, is_l...]
  transfers between devices with their start and end apart: 4 -> 4, of which waited for: 4 -> 1; matrix products, arithmetic and copies ran while one was open for 7% -> 7% of each run, Pallas kernels for 62% -> 69%
where the time goes in v4:
time: 446 us
  Pallas kernels  347 us (78%)
  waiting for transfers between devices  48.6 us (11%)
  other arithmetic  24.8 us (6%)
  between operations  13.4 us (3%)
  local copies, waits for them, and re-layouts  11.7 us (3%)
    pallas_call x4, Pallas kernels, moe_call(): pl.pallas_call(functools.partial(moe_kernel, first_expert, is_first, is_l...  245 us
    pallas_call x1, Pallas kernels, attend_call(): pl.pallas_call(functools.partial(attend_kernel, head_dim), grid=(kv_heads...  74 us
    all_gather x1, waiting for transfers between devices, device_step(): head = lax.all_gather(stacks[0], 'ep', axis=0, tiled=False)  47.3 us
    pallas_call x1, Pallas kernels, qkv_call(): pl.pallas_call(functools.partial(qkv_kernel, head_dim, q_cols, k_cols), g...  15.4 us
    pallas_call x1, Pallas kernels, out_call(): pl.pallas_call(out_kernel, grid=(tokens // rows,), in_specs=[pl.BlockSpec...  11.8 us
  transfers between devices with their start and end apart: 4, of which 1 were waited for; matrix products, arithmetic and copies ran while one was open for 7% of the time, Pallas kernels for 69%

profile of v4, /device:TPU:97, one launch (start us, length us, event | category | flops | bytes accessed | tf_op | source)
XLA Modules:
  0.0 445.7 jit_solution(7731964659845023378)
XLA Ops:
  6.6 1.2 reshape.48
  7.8 1.1 reshape.49
  9.0 0.8 bitcast_dynamic-update-slice_fusion.1
  9.7 0.8 bitcast_dynamic-update-slice_fusion
  10.5 0.9 slice_dynamic-update-slice_fusion.2
  11.4 0.9 slice_dynamic-update-slice_fusion.1
  12.3 0.9 slice_dynamic-update-slice_fusion
  13.3 0.8 copy-done
  14.2 1.1 slice.168
  15.4 1.0 slice.169
  16.4 0.9 slice.170
  17.4 0.6 broadcast_in_dim.256.gain_ref
  18.0 0.6 broadcast_in_dim.257.gain_ref
  18.6 0.8 pad_maximum_fusion.2
  19.4 1.0 pad_maximum_fusion.1
  20.5 1.2 pad_maximum_fusion
  21.8 0.1 slice_convert_fusion.15
  21.9 1.0 select_select_fusion.2.slot_row_ref
  22.9 7.9 %select_select_fusion.slot_ref = f32[2048,128]{1,0:T(8,128)} fusion(f32[2048]{0:T(1024)S(1)} %bitcast.140, f32[2048]{0:T(1024)S(1)} %bitcast.139, f32[2048]{0:T(1024)S(1)} %bitcast.138, f32[2048]{0:T(1024)S(1)} %bitcast.137, f32[2048]{0:T(1024)S(1)} %bitcast.136, f32[2048]{0:T(1024)S(1)} %bitcast.135, f32[2048]{0:T(1024)S(1)} %bitcast.134, ...), kind=kLoop, calls=%fused_computation.1 | loop fusion | flops 8388608 | bytes 1245696 | tf_op jit(solution)/shard_map/jit(_where)/select_n | solution.py:401
  30.8 7.9 %select_select_fusion.1.gate_ref = f32[2048,128]{1,0:T(8,128)} fusion(f32[2048]{0:T(1024)S(1)} %bitcast.126, s32[2048]{0:T(1024)S(1)} %bitcast.79, f32[2048]{0:T(1024)S(1)} %bitcast.127, s32[2048]{0:T(1024)S(1)} %bitcast.82, f32[2048]{0:T(1024)S(1)} %bitcast.128, s32[2048]{0:T(1024)S(1)} %bitcast.85, f32[2048]{0:T(1024)S(1)} %bitcast.129, ...), kind=kLoop, calls=%fused_computation.2 | loop fusion | flops 8388608 | bytes 1245696 | tf_op jit(solution)/shard_map/jit(_where)/select_n | solution.py:400
  38.7 4.8 %sine_multiply_fusion = (f32[2048,128]{1,0:T(8,128)}, f32[2048,128]{1,0:T(8,128)}) fusion(f32[128]{0:T(128)S(1)} %get-tuple-element.73, f32[128]{0:T(128)S(1)} %get-tuple-element.74), kind=kLoop, calls=%fused_computation.11 | loop fusion | flops 524288 | bytes 2098176 | tf_op jit(solution)/shard_map/mul | solution.py:412
  43.5 47.3 %all-gather.9.cloned.1.call-done = bf16[576,32,512]{2,1,0:T(8,128)(2,1)} async-done(((bf16[18,32,512]{2,1,0:T(8,128)(2,1)}), bf16[576,32,512]{2,1,0:T(8,128)(2,1)}) %all-gather.9.cloned.1.call-update) | async-done | bytes 18874384 | tf_op jit(solution)/shard_map/all_gather | solution.py:455
  90.9 0.7 all-gather.13.cloned.1.call-update
  91.7 0.2 all-gather.11.cloned.1.call-start
  91.9 0.4 all-gather.11.cloned.1.call-update
  92.3 15.4 %qkv_rope.1 = (bf16[2048,1024]{1,0:T(8,128)(2,1)}, bf16[2,2048,512]{2,1,0:T(8,128)(2,1)}, bf16[2,2048,512]{2,1,0:T(8,128)(2,1)}) custom-call(bf16[2048,1024]{1,0:T(8,128)(2,1)} %bitcast.68, bf16[1,1024]{1,0:T(2,128)(2,1)} %broadcast_in_dim.256.gain_ref, bf16[32,18,32,512]{3,2,1,0:T(8,128)(2,1)} %bitcast.63, f32[2048,128]{1,0:T(8,128)} %get-tuple-element.25.cos_ref, ...), custom_call_target="tpu_custom_call" | custom-call | flops 8589934592 | bytes 20971520 | tf_op jit(solution)/shard_map/qkv_rope/pallas_call | solution.py:84
  107.7 74.0 %attend.1.mixed_ref = bf16[2048,1024]{1,0:T(8,128)(2,1)} custom-call(bf16[2048,1024]{1,0:T(8,128)(2,1)} %get-tuple-element.27.q_ref, bf16[2,2048,512]{2,1,0:T(8,128)(2,1)} %get-tuple-element.28.ka_ref.kb_ref, bf16[2,2048,512]{2,1,0:T(8,128)(2,1)} %get-tuple-element.28.ka_ref.kb_ref, bf16[2,2048,512]{2,1,0:T(8,128)(2,1)} %get-tuple-element.29.va_ref.vb_ref, ...), custom_call_target="tpu_custom_call" | custom-call | flops 34359738368 | bytes 25165824 | tf_op jit(solution)/shard_map/attend/pallas_call | solution.py:199
  181.7 11.8 %out_proj.1 = (bf16[2048,1024]{1,0:T(8,128)(2,1)}, bf16[2048,1024]{1,0:T(8,128)(2,1)}) custom-call(bf16[2048,1024]{1,0:T(8,128)(2,1)} %attend.1.mixed_ref, bf16[32,18,32,512]{3,2,1,0:T(8,128)(2,1)} %bitcast.64, bf16[2048,1024]{1,0:T(8,128)(2,1)} %bitcast.69, bf16[1,1024]{1,0:T(2,128)(2,1)} %broadcast_in_dim.257.gain_ref), custom_call_target="tpu_custom_call" | custom-call | flops 4294967296 | bytes 20971520 | tf_op jit(solution)/shard_map/out_proj/pallas_call | solution.py:236
  193.6 37.5 %moe_part.4.rest_0_ = f32[2048,1024]{1,0:T(8,128)} custom-call(s32[32]{0:T(128)} %bitcast.141, bf16[2048,1024]{1,0:T(8,128)(2,1)} %get-tuple-element.31.u_ref, f32[2048,128]{1,0:T(8,128)} %select_select_fusion.1.gate_ref, f32[2048,128]{1,0:T(8,128)} %select_select_fusion.slot_ref, s32[32,2048]{1,0:T(8,128)} %select_select_fusion.2.slot_row_ref, ...), custom_call_target="tpu_custom_call" | custom-call | flops 25769803776 | bytes 52428800 | tf_op jit(solution)/shard_map/moe_part/pallas_call | solution.py:375
  231.1 99.5 %moe_part.5.rest_0_ = f32[2048,1024]{1,0:T(8,128)} custom-call(s32[32]{0:T(128)} %bitcast.142, bf16[2048,1024]{1,0:T(8,128)(2,1)} %get-tuple-element.31.u_ref, f32[2048,128]{1,0:T(8,128)} %select_select_fusion.1.gate_ref, f32[2048,128]{1,0:T(8,128)} %select_select_fusion.slot_ref, s32[32,2048]{1,0:T(8,128)} %select_select_fusion.2.slot_row_ref, ...), custom_call_target="tpu_custom_call" | custom-call | flops 90194313216 | bytes 77594624 | tf_op jit(solution)/shard_map/moe_part/pallas_call | solution.py:375
  330.6 67.7 %moe_part.6.rest_0_ = f32[2048,1024]{1,0:T(8,128)} custom-call(s32[32]{0:T(128)} %bitcast.143, bf16[2048,1024]{1,0:T(8,128)(2,1)} %get-tuple-element.31.u_ref, f32[2048,128]{1,0:T(8,128)} %select_select_fusion.1.gate_ref, f32[2048,128]{1,0:T(8,128)} %select_select_fusion.slot_ref, s32[32,2048]{1,0:T(8,128)} %select_select_fusion.2.slot_row_ref, ...), custom_call_target="tpu_custom_call" | custom-call | flops 57982058496 | bytes 61865984 | tf_op jit(solution)/shard_map/moe_part/pallas_call | solution.py:375
  398.4 40.7 %moe_part.7 = bf16[2048,1024]{1,0:T(8,128)(2,1)} custom-call(s32[32]{0:T(128)} %bitcast.144, bf16[2048,1024]{1,0:T(8,128)(2,1)} %get-tuple-element.31.u_ref, f32[2048,128]{1,0:T(8,128)} %select_select_fusion.1.gate_ref, f32[2048,128]{1,0:T(8,128)} %select_select_fusion.slot_ref, s32[32,2048]{1,0:T(8,128)} %select_select_fusion.2.slot_row_ref, ...), custom_call_target="tpu_custom_call" | custom-call | flops 32212254720 | bytes 49283072 | tf_op jit(solution)/shard_map/moe_part/pallas_call | solution.py:375
  (41 shorter events, 0.6 us)
Async XLA Ops:
  6.5 12.0 %slice-start.2 = ((bf16[32,32,512]{2,1,0:T(8,128)(2,1)}), bf16[5,32,512]{2,1,0:T(8,128)(2,1)S(1)}, s32[]{:S(2)}) async-start(bf16[32,32,512]{2,1,0:T(8,128)(2,1)} %param.19), calls=%async_computation.6 | async-start | bytes 327680 | tf_op jit(solution)/shard_map/slice | solution.py:451
  6.5 12.0 %slice-start.5 = ((bf16[32,32,512]{2,1,0:T(8,128)(2,1)}), bf16[5,32,512]{2,1,0:T(8,128)(2,1)S(1)}, s32[]{:S(2)}) async-start(bf16[32,32,512]{2,1,0:T(8,128)(2,1)} %param.20), calls=%async_computation.9 | async-start | bytes 327680 | tf_op jit(solution)/shard_map/slice | solution.py:451
  6.6 10.8 %copy-start.4 = (bf16[1024]{0:T(1024)(128)(2,1)S(1)}, bf16[1024]{0:T(1024)(128)(2,1)}, u32[]{:S(2)}) copy-start(bf16[1024]{0:T(1024)(128)(2,1)} %param.17) | copy-start | bytes 6148
  6.6 11.4 %copy-start.5 = (bf16[1024]{0:T(1024)(128)(2,1)S(1)}, bf16[1024]{0:T(1024)(128)(2,1)}, u32[]{:S(2)}) copy-start(bf16[1024]{0:T(1024)(128)(2,1)} %param.18) | copy-start | bytes 6148
  6.6 12.0 %copy-start.6 = (s32[1,32]{1,0:T(1,128)S(1)}, s32[1,32]{1,0:T(1,128)}, u32[]{:S(2)}) copy-start(s32[1,32]{1,0:T(1,128)} %param.24) | copy-start | bytes 388
  6.6 84.2 %all-gather.9.cloned.1.call-start = ((), (), s32[]{:S(2)}) async-start(), calls=%async_computation | async-start | bytes 19464192 | tf_op jit(solution)/shard_map/all_gather | solution.py:455
  7.8 11.6 %slice-start.1 = ((bf16[32,32,512]{2,1,0:T(8,128)(2,1)}), bf16[9,32,512]{2,1,0:T(8,128)(2,1)S(1)}, s32[]{:S(2)}) async-start(bf16[32,32,512]{2,1,0:T(8,128)(2,1)} %param.19), calls=%async_computation.5 | async-start | bytes 589824 | tf_op jit(solution)/shard_map/slice | solution.py:451
  7.8 11.6 %slice-start.4 = ((bf16[32,32,512]{2,1,0:T(8,128)(2,1)}), bf16[9,32,512]{2,1,0:T(8,128)(2,1)S(1)}, s32[]{:S(2)}) async-start(bf16[32,32,512]{2,1,0:T(8,128)(2,1)} %param.20), calls=%async_computation.8 | async-start | bytes 589824 | tf_op jit(solution)/shard_map/slice | solution.py:451
  13.3 0.8 copy-start
  14.1 6.3 %slice-start = ((bf16[32,32,512]{2,1,0:T(8,128)(2,1)}), bf16[14,32,512]{2,1,0:T(8,128)(2,1)S(1)}, s32[]{:S(2)}) async-start(bf16[32,32,512]{2,1,0:T(8,128)(2,1)} %param.19), calls=%async_computation.4 | async-start | bytes 917504 | tf_op jit(solution)/shard_map/slice | solution.py:451
  14.1 6.3 %slice-start.3 = ((bf16[32,32,512]{2,1,0:T(8,128)(2,1)}), bf16[14,32,512]{2,1,0:T(8,128)(2,1)S(1)}, s32[]{:S(2)}) async-start(bf16[32,32,512]{2,1,0:T(8,128)(2,1)} %param.20), calls=%async_computation.7 | async-start | bytes 917504 | tf_op jit(solution)/shard_map/slice | solution.py:451
  14.2 216.9 %all-gather.15.cloned.1.call-start = ((), (), s32[]{:S(2)}) async-start(), calls=%async_computation.3 | async-start | bytes 45416448 | tf_op jit(solution)/shard_map/all_gather | solution.py:460
  15.4 6.3 %copy-start.1 = (bf16[1,2048,8]{1,2,0:T(8,128)(2,1)S(1)}, bf16[1,2048,8]{1,2,0:T(8,128)(2,1)}, u32[]{:S(2)}) copy-start(bf16[1,2048,8]{1,2,0:T(8,128)(2,1)} %param.25) | copy-start | bytes 98308
  15.4 6.4 %copy-start.3 = (s32[1,2048,8]{1,2,0:T(8,128)S(1)}, s32[1,2048,8]{1,2,0:T(8,128)}, u32[]{:S(2)}) copy-start(s32[1,2048,8]{1,2,0:T(8,128)} %param.22) | copy-start | bytes 196612
  15.4 6.4 %copy-start.2 = (s32[1,2048,8]{1,2,0:T(8,128)S(1)}, s32[1,2048,8]{1,2,0:T(8,128)}, u32[]{:S(2)}) copy-start(s32[1,2048,8]{1,2,0:T(8,128)} %param.23) | copy-start | bytes 196612
  90.9 239.8 %all-gather.13.cloned.1.call-start = ((), (), s32[]{:S(2)}) async-start(), calls=%async_computation.2 | async-start | bytes 29196288 | tf_op jit(solution)/shard_map/all_gather | solution.py:460
  91.7 306.7 %all-gather.11.cloned.1.call-start = ((), (), s32[]{:S(2)}) async-start(), calls=%async_computation.1 | async-start | bytes 16220160 | tf_op jit(solution)/shard_map/all_gather | solution.py:460
Sparse Core Ops, SparseCore 0:
  14.3 76.4 all-gather.8
  92.9 135.2 all-gather.14
  230.2 93.7 all-gather.12
  326.0 63.9 all-gather.10
